TPU v7x, 8 devices: a whole 2x2x1 slice. The times are simulated.
8 devices in a mesh: dp: 1 (over z), ei: 2 (over y), eo: 4 (over x, core).
Axes of the slice: x: 2, y: 2, z: 1, core: 2. Of those that a mesh axis runs over, the one named last changes fastest.
Arguments:
- tokens: bfloat16 [512, 2048], P(('dp', 'ei', 'eo'))
- expert_idx: int32 [512, 6], P(('dp', 'ei', 'eo'))
- gates: float32 [512, 6], P(('dp', 'ei', 'eo'))
- w_gate: bfloat16 [32, 2048, 1408], P(('ei', 'eo'))
- w_up: bfloat16 [32, 2048, 1408], P(('ei', 'eo'))
- w_down: bfloat16 [32, 1408, 2048], P(('ei', 'eo'))
- grad_out: bfloat16 [512, 2048], P(('dp', 'ei', 'eo'))
Outputs:
- output 1: bfloat16 [512, 2048], P(('dp', 'ei', 'eo'))
- output 2: bfloat16 [512, 2048], P(('dp', 'ei', 'eo'))
- output 3: float32 [512, 6], P(('dp', 'ei', 'eo'))
- output 4: bfloat16 [32, 2048, 1408], P(('dp', 'ei', 'eo'))
- output 5: bfloat16 [32, 2048, 1408], P(('dp', 'ei', 'eo'))
- output 6: bfloat16 [32, 1408, 2048], P(('dp', 'ei', 'eo'))
All inputs are finite; a program needn't handle non-finite values.
Results may differ from a plain program's by a relative error of at most 0.00167.
Values are sent between devices in bfloat16 or wider.
A program may use at most 1 GiB of HBM per device.

v0:
```python
import functools

import jax
import jax.numpy as jnp
from jax import lax
from jax.experimental import pallas as pl
from jax.experimental.pallas import tpu as pltpu
from jax.sharding import PartitionSpec as P


F32 = jnp.float32
BF16 = jnp.bfloat16
MESH = pl.DeviceIdType.MESH

TD = 64
D = 2048
F = 1408
K = 6
E = 4
CAP = 24
ND = 8
ROWS = ND * CAP

NT = (((1,), (1,)), ((), ()))
TN = (((0,), (0,)), ((), ()))


def dot(a, b, dims=None):
    if dims is None:
        return jnp.dot(a, b, preferred_element_type=F32)
    return lax.dot_general(a, b, dims, preferred_element_type=F32)


def place():
    y = lax.axis_index('ei')
    o = lax.axis_index('eo')
    x = o // 2
    c = o % 2
    return y, x, c


def flip_if(v, f):
    return v + f - 2 * v * f


def main_kernel(x_hbm, dy_hbm, tbl_hbm, wg_hbm, wu_hbm, wd_hbm,
                y_out, dgt_out, s1_out, k1_out, xs_out, us_out, hs_out, dgu_out,
                wgu, wd, xall, dyall, tall, rk, gt, ab, oall, py, rb0, rb1, rb2,
                dgs, dgr, xsb, usb, hsb, dgb,
                wsem, lsem, snd, rcv, rs_s, rs_r, dg_s, dg_r, osem, psem, credit):
    dp = lax.axis_index('dp')
    y, x, c = place()
    chip = y * 2 + x
    me = chip * 2 + c
    yp, xp = flip_if(y, c), flip_if(x, 1 - c)
    ys, xs = flip_if(y, 1 - c), flip_if(x, c)
    cp, cs, cd = yp * 2 + xp, ys * 2 + xs, (1 - y) * 2 + (1 - x)

    def dev(yy, xx, cc):
        return (dp, yy, xx * 2 + cc)

    partner, prim, sec = dev(y, x, 1 - c), dev(yp, xp, c), dev(ys, xs, c)

    def rcopy(src, dst, ss, rs, target):
        return pltpu.make_async_remote_copy(src_ref=src, dst_ref=dst, send_sem=ss, recv_sem=rs,
                                            device_id=target, device_id_type=MESH)

    def load(src, dst, sem):
        return pltpu.make_async_copy(src, dst, sem)

    def weight_copies(e, sl):
        return (load(wg_hbm.at[e], wgu.at[sl, :, pl.ds(0, F)], wsem.at[sl, 0]),
                load(wu_hbm.at[e], wgu.at[sl, :, pl.ds(F, F)], wsem.at[sl, 1]),
                load(wd_hbm.at[e], wd.at[sl], wsem.at[sl, 2]))

    ins = (load(x_hbm, xall.at[me], lsem.at[0]), load(tbl_hbm, tall.at[me], lsem.at[1]),
           load(dy_hbm, dyall.at[me], lsem.at[2]))
    for cpy in ins:
        cpy.start()
    for e in range(2):
        for cpy in weight_copies(e, e):
            cpy.start()

    barrier = pltpu.get_barrier_semaphore()
    others = [lax.rem(me + k, ND) for k in range(1, ND)]
    for t in others:
        pl.semaphore_signal(barrier, inc=1, device_id=(dp, t // 4, lax.rem(t, 4)), device_id_type=MESH)
    pl.semaphore_wait(barrier, ND - 1)

    bufs = (xall, tall, dyall)
    me_p, me_s, me_d = cp * 2 + c, cs * 2 + c, cd * 2 + c

    def ag_send(st, chunk, k, r, target):
        buf = bufs[st]
        return rcopy(buf.at[chunk], buf.at[chunk], snd.at[st, k], rcv.at[st, r], target)

    def ag_wait(st, chunk, r):
        ag_send(st, chunk, 0, r, partner).wait_recv()

    def ag_open(st):
        ag_send(st, me, 0, 0, prim).start()
        ag_send(st, me, 1, 1, sec).start()
        ag_send(st, me, 2, 3, partner).start()

    def ag_first(st):
        ag_wait(st, me_p, 0)
        ag_send(st, me_p, 3, 2, sec).start()
        ag_send(st, me_p, 4, 5, partner).start()

    def ag_rest(st):
        ag_wait(st, me_s, 1)
        ag_send(st, me_s, 5, 4, partner).start()
        ag_wait(st, me_d, 2)
        ag_send(st, me_d, 6, 6, partner).start()

    def ag_last(st):
        oc = 1 - c
        ag_wait(st, chip * 2 + oc, 3)
        ag_wait(st, cp * 2 + oc, 4)
        ag_wait(st, cs * 2 + oc, 5)
        ag_wait(st, cd * 2 + oc, 6)

    def ag_sent(st):
        for k, (chunk, target) in enumerate(((me, prim), (me, sec), (me, partner), (me_p, sec),
                                             (me_p, partner), (me_s, partner), (me_d, partner))):
            ag_send(st, chunk, k, 0, target).wait_send()

    ins[1].wait()
    ag_open(1)
    ins[0].wait()
    ag_open(0)
    ins[2].wait()
    ag_first(1)
    ag_rest(1)
    ag_first(0)
    ag_last(1)

    li = lax.broadcasted_iota(jnp.int32, (128, 128), 0)
    lj = lax.broadcasted_iota(jnp.int32, (128, 128), 1)
    upper = jnp.where((li // TD == lj // TD) & (li < lj), 1.0, 0.0).astype(BF16)
    for p in range(4):
        tb = tall[2 * p] + tall[2 * p + 1]
        ids, gv = tb[0:8], tb[8:16]
        for e in range(E):
            eid = (me * E + e).astype(F32)
            eq = ids == eid
            hit = jnp.sum(jnp.where(eq, 1.0, 0.0), axis=0, keepdims=True)
            gate = jnp.sum(jnp.where(eq, gv, 0.0), axis=0, keepdims=True)
            hit8 = jnp.broadcast_to(hit, (8, 128))
            rank = dot(hit8.astype(BF16), upper)
            rk[e, :, 128 * p:128 * (p + 1)] = jnp.where(hit8 > 0.5, rank, -1000.0)
            gt[e, :, 128 * p:128 * (p + 1)] = jnp.broadcast_to(gate, (8, 128))

    tok = lax.broadcasted_iota(jnp.int32, (1, ND * TD), 1)
    slot_base = (tok // TD * CAP).astype(F32)
    slot_row = lax.broadcasted_iota(jnp.int32, (ROWS, ND * TD), 0).astype(F32)

    def slot_mask(e):
        return (rk[e][0:1, :] + slot_base) == slot_row

    def put_rows(e, c0, width, val):
        for s in range(ND):
            oall[s, e, :, c0:c0 + width] = val[s * CAP:(s + 1) * CAP]

    ag_rest(0)
    ag_open(2)
    ag_last(0)

    def fwd(e, carry):
        sl = lax.rem(e, 2)
        sel = jnp.where(slot_mask(e), 1.0, 0.0).astype(BF16)

        @pl.when(e > 0)
        def _():
            load(xsb, xs_out.at[e], osem.at[0]).wait()
            load(hsb, hs_out.at[e], osem.at[1]).wait()

        for n in range(4):
            xsb[:, 512 * n:512 * (n + 1)] = dot(sel, xall[:, :, 512 * n:512 * (n + 1)].reshape(ND * TD, 512)).astype(BF16)
        load(xsb, xs_out.at[e], osem.at[0]).start()
        cg, cu, cw = weight_copies(e, sl)
        cg.wait()
        cu.wait()
        for n in range(6):
            lo, w = 256 * n, 256 if n < 5 else 128
            if w == 256:
                a = dot(xsb[...], wgu[sl, :, lo:lo + w])
                b = dot(xsb[...], wgu[sl, :, F + lo:F + lo + w])
            else:
                rhs = jnp.concatenate([wgu[sl, :, lo:lo + w], wgu[sl, :, F + lo:F + lo + w]], axis=1)
                r = dot(xsb[...], rhs)
                a, b = r[:, :w], r[:, w:]
            ab[e, :, lo:lo + w] = a
            ab[e, :, F + lo:F + lo + w] = b
            hsb[:, lo:lo + w] = (a * jax.nn.sigmoid(a) * b).astype(BF16)
        load(hsb, hs_out.at[e], osem.at[1]).start()

        @pl.when(e < 2)
        def _():
            for cpy in weight_copies(e + 2, sl)[:2]:
                cpy.start()

        cw.wait()
        for n in range(8):
            put_rows(e, 256 * n, 256, dot(hsb[...], wd[sl, :, 256 * n:256 * (n + 1)]).astype(BF16))

        @pl.when(e < 2)
        def _():
            weight_copies(e + 2, sl)[2].start()

        @pl.when(e == 1)
        def _():
            ag_first(2)

        @pl.when(e == 2)
        def _():
            ag_rest(2)

        return carry

    lax.fori_loop(0, E, fwd, 0)
    load(xsb, xs_out.at[E - 1], osem.at[0]).wait()
    load(hsb, hs_out.at[E - 1], osem.at[1]).wait()
    ag_last(2)

    krow = lax.broadcasted_iota(jnp.int32, (2 * E * CAP, 128), 0).astype(F32)
    ptok = lax.broadcasted_iota(jnp.int32, (1, 128), 1)
    pbase = (ptok // TD * (E * CAP)).astype(F32)

    def scatter(gated, put):
        def body(p, carry):
            sel = jnp.zeros((2 * E * CAP, 128), F32)
            lanes = pl.ds(pl.multiple_of(p * 128, 128), 128)
            for e in range(E):
                m = (rk[e, :, lanes][0:1, :] + pbase + float(e * CAP)) == krow
                sel = jnp.where(m, gt[e, :, lanes][0:1, :] if gated else 1.0, sel)
            if gated:
                g1 = sel.astype(BF16)
                r1 = sel - g1.astype(F32)
                g2 = r1.astype(BF16)
                g3 = (r1 - g2.astype(F32)).astype(BF16)
                lhs = jnp.concatenate([g1, g2, g3], axis=1)
            else:
                lhs = sel.astype(BF16)
            for n in range(4):
                rhs = oall[pl.ds(2 * p, 2), :, :, 512 * n:512 * (n + 1)].reshape(2 * E * CAP, 512)
                r = dot(lhs, rhs, TN)
                if gated:
                    r = r[0:128] + (r[128:256] + r[256:384])
                put(p, slice(512 * n, 512 * (n + 1)), r)
            return carry

        lax.fori_loop(0, 4, body, 0)

    def put_y(p, cols, r):
        py[0, p, :, cols] = r[0:TD]
        py[1, p, :, cols] = r[TD:]

    scatter(True, put_y)

    rs0 = rcopy(py.at[1 - c], rb0, rs_s.at[0], rs_r.at[0], partner)
    rs1a = rcopy(py.at[c, cd], rb1.at[1], rs_s.at[1], rs_r.at[1], prim)
    rs1b = rcopy(py.at[c, cp], rb1.at[0], rs_s.at[2], rs_r.at[2], prim)
    rs2 = rcopy(py.at[c, cs], rb2, rs_s.at[3], rs_r.at[3], sec)
    rs0.start()

    def bwd(n, carry):
        e = E - 1 - n
        sl = lax.rem(e, 2)
        mask = slot_mask(e)
        sel = jnp.where(mask, 1.0, 0.0).astype(BF16)
        gcol = jnp.sum(jnp.where(mask, gt[e][0:1, :], 0.0), axis=1, keepdims=True)

        @pl.when(n > 0)
        def _():
            load(usb, us_out.at[e], osem.at[0]).wait()
            load(dgb, dgu_out.at[e], osem.at[1]).wait()

        dgv = jnp.zeros((ROWS, 1), F32)
        for m in range(4):
            c0 = 512 * m
            dye = dot(sel, dyall[:, :, c0:c0 + 512].reshape(ND * TD, 512))
            usb[:, c0:c0 + 512] = (gcol * dye).astype(BF16)
            oe = jnp.concatenate([oall[s, e, :, c0:c0 + 512] for s in range(ND)], axis=0).astype(F32)
            dgv = dgv + jnp.sum(dye * oe, axis=1, keepdims=True)
        dgrow = jnp.sum(jnp.where(mask, dgv, 0.0), axis=0, keepdims=True)
        dgs[e] = jnp.broadcast_to(dgrow, (8, ND * TD))
        load(usb, us_out.at[e], osem.at[0]).start()
        cg, cu, cw = weight_copies(e, sl)

        @pl.when(n >= 2)
        def _():
            cw.wait()

        for lo, hi in ((0, 768), (768, F)):
            q = dot(wd[sl, lo:hi, :], usb[...], NT).T
            a = ab[e, :, lo:hi]
            b = ab[e, :, F + lo:F + hi]
            s = jax.nn.sigmoid(a)
            dgb[:, F + lo:F + hi] = (q * a * s).astype(BF16)
            dgb[:, lo:hi] = (q * b * s * (1.0 + a * (1.0 - s))).astype(BF16)
        load(dgb, dgu_out.at[e], osem.at[1]).start()

        @pl.when(n < 2)
        def _():
            weight_copies(1 - n, sl)[2].start()

        @pl.when(n == 2)
        def _():
            rs1a.wait_recv()
            py[c, cs] = py[c, cs] + rb1[1]
            rs2.start()

        @pl.when(n >= 2)
        def _():
            cg.wait()
            cu.wait()

        for m in range(4):
            dxt = dot(wgu[sl, 512 * m:512 * (m + 1), :], dgb[...], NT)
            put_rows(e, 512 * m, 512, dxt.T.astype(BF16))

        @pl.when(n < 2)
        def _():
            for cpy in weight_copies(1 - n, sl)[:2]:
                cpy.start()

        @pl.when(n == 0)
        def _():
            rs0.wait()
            py[c] = py[c] + rb0[...]
            rs1a.start()
            rs1b.start()
            pl.semaphore_signal(credit, inc=1, device_id=partner, device_id_type=MESH)

        return carry

    lax.fori_loop(0, E, bwd, 0)
    load(usb, us_out.at[0], osem.at[0]).wait()
    load(dgb, dgu_out.at[0], osem.at[1]).wait()

    sends = []
    for i, t in enumerate(others):
        lanes = pl.ds(pl.multiple_of(t // 2 * 128, 128), 128)
        cpy = rcopy(dgs.at[:, :, lanes], dgr.at[me], dg_s.at[i], dg_r.at[me],
                    (dp, t // 4, lax.rem(t, 4)))
        cpy.start()
        sends.append(cpy)
    dgr[me] = dgs[:, :, pl.ds(pl.multiple_of(chip * 128, 128), 128)]

    def put_dx(p, cols, r):
        ab[p, 0:2 * TD, cols] = r

    scatter(False, put_dx)
    pl.semaphore_wait(credit, 1)
    dx0 = rcopy(ab.at[:, pl.ds(pl.multiple_of((1 - c) * TD, TD), TD), pl.ds(0, D)], rb0,
                rs_s.at[4], rs_r.at[4], partner)
    dx0.start()

    rs1b.wait_recv()
    rs2.wait_recv()
    y_out[...] = (py[c, chip] + rb1[0] + rb2[...]).astype(BF16)

    for i, t in enumerate(others):
        rcopy(dgs.at[:, :, pl.ds(0, 128)], dgr.at[t], dg_s.at[i], dg_r.at[t], partner).wait_recv()
    tb = tall[2 * chip] + tall[2 * chip + 1]
    ids = tb[0:8]
    acc = jnp.zeros((8, 128), F32)
    for t in range(ND):
        for e in range(E):
            acc = acc + jnp.where(ids == float(t * E + e), dgr[t, e], 0.0)
    dgt_out[...] = acc

    dx0.wait_recv()
    own_rows = pl.ds(pl.multiple_of(c * TD, TD), TD)
    parts = []
    for i, (k, out) in enumerate(((cp, s1_out.at[0]), (cd, s1_out.at[1]), (chip, k1_out.at[0]), (cs, k1_out.at[1]))):
        ab[i, 2 * TD:3 * TD, 0:D] = ab[k, own_rows, 0:D] + rb0[k]
        cpy = load(ab.at[i, pl.ds(2 * TD, TD), pl.ds(0, D)], out, psem.at[i])
        cpy.start()
        parts.append(cpy)

    dx0.wait_send()
    rs1a.wait_send()
    rs1b.wait_send()
    rs2.wait_send()
    for st in range(3):
        ag_sent(st)
    for cpy in sends:
        cpy.wait_send()
    for cpy in parts:
        cpy.wait()


def run_main(tok, dy, tbl, wg, wu, wd):
    anys = pl.BlockSpec(memory_space=pl.ANY)
    vm = pl.BlockSpec(memory_space=pltpu.VMEM)
    V = pltpu.VMEM
    S = pltpu.SemaphoreType.DMA
    flops = 2 * E * ROWS * D * F * 6
    return pl.pallas_call(
        main_kernel,
        name='moe_main',
        out_shape=(jax.ShapeDtypeStruct((TD, D), BF16), jax.ShapeDtypeStruct((8, 128), F32),
                   jax.ShapeDtypeStruct((2, TD, D), F32), jax.ShapeDtypeStruct((2, TD, D), F32),
                   jax.ShapeDtypeStruct((E, ROWS, D), BF16), jax.ShapeDtypeStruct((E, ROWS, D), BF16),
                   jax.ShapeDtypeStruct((E, ROWS, F), BF16), jax.ShapeDtypeStruct((E, ROWS, 2 * F), BF16)),
        in_specs=[anys] * 6,
        out_specs=(vm, vm) + (anys,) * 6,
        scratch_shapes=[
            V((2, D, 2 * F), BF16), V((2, F, D), BF16),
            V((ND, TD, D), BF16), V((ND, TD, D), BF16), V((ND, 16, 128), F32),
            V((E, 8, ND * TD), F32), V((E, 8, ND * TD), F32),
            V((E, ROWS, 2 * F), F32), V((ND, E, CAP, D), BF16),
            V((2, 4, TD, D), F32), V((4, TD, D), F32), V((2, TD, D), F32), V((TD, D), F32),
            V((E, 8, ND * TD), F32), V((ND, E, 8, 128), F32),
            V((ROWS, D), BF16), V((ROWS, D), BF16), V((ROWS, F), BF16), V((ROWS, 2 * F), BF16),
            S((2, 3)), S((3,)), S((3, 7)), S((3, 7)), S((5,)), S((5,)), S((7,)), S((ND,)), S((2,)), S((4,)),
            pltpu.SemaphoreType.REGULAR,
        ],
        compiler_params=pltpu.CompilerParams(collective_id=0, has_side_effects=True,
                                             vmem_limit_bytes=67043328),
        cost_estimate=pl.CostEstimate(flops=flops, bytes_accessed=120_000_000, transcendentals=0),
    )(tok, dy, tbl, wg, wu, wd)


RING = 4


def ring_loop(steps, ring, outs, compute):
    def body(i, carry):
        slot = lax.rem(i, ring)

        @pl.when(i >= ring)
        def _():
            for cpy in outs(i - ring, slot):
                cpy.wait()

        compute(i, slot)
        for cpy in outs(i, slot):
            cpy.start()
        return carry

    lax.fori_loop(0, steps, body, 0)
    for k in range(ring):
        i = steps - ring + k
        for cpy in outs(i, i % ring):
            cpy.wait()


def gate_up_kernel(x_hbm, g_hbm, og_hbm, ou_hbm, x_v, g_v, og_v, ou_v, isem, osem):
    def ins(e):
        return (pltpu.make_async_copy(x_hbm.at[e], x_v.at[e], isem.at[e, 0]),
                pltpu.make_async_copy(g_hbm.at[e], g_v.at[e], isem.at[e, 1]))

    for e in range(E):
        for cpy in ins(e):
            cpy.start()

    def outs(i, slot):
        rows = pl.ds(pl.multiple_of(lax.rem(i, 4) * 512, 512), 512)
        return (pltpu.make_async_copy(og_v.at[slot], og_hbm.at[i // 4, rows], osem.at[slot, 0]),
                pltpu.make_async_copy(ou_v.at[slot], ou_hbm.at[i // 4, rows], osem.at[slot, 1]))

    def compute(i, slot):
        e = i // 4

        @pl.when(lax.rem(i, 4) == 0)
        def _():
            for cpy in ins(e):
                cpy.wait()

        cols = pl.ds(pl.multiple_of(lax.rem(i, 4) * 512, 512), 512)
        r = dot(x_v[e, :, cols], g_v[e], TN)
        og_v[slot] = r[:, :F].astype(BF16)
        ou_v[slot] = r[:, F:].astype(BF16)

    ring_loop(4 * E, RING, outs, compute)


def run_gate_up(xs, dgu):
    anys = pl.BlockSpec(memory_space=pl.ANY)
    V = pltpu.VMEM
    return pl.pallas_call(
        gate_up_kernel, name='moe_dw_gate_up',
        in_specs=[anys, anys], out_specs=(anys, anys),
        out_shape=(jax.ShapeDtypeStruct((E, D, F), BF16),) * 2,
        scratch_shapes=[V((E, ROWS, D), BF16), V((E, ROWS, 2 * F), BF16),
                        V((RING, 512, F), BF16), V((RING, 512, F), BF16),
                        pltpu.SemaphoreType.DMA((E, 2)), pltpu.SemaphoreType.DMA((RING, 2))],
        compiler_params=pltpu.CompilerParams(vmem_limit_bytes=67043328),
        cost_estimate=pl.CostEstimate(flops=4 * E * ROWS * D * F, bytes_accessed=55_000_000, transcendentals=0),
    )(xs, dgu)


def down_kernel(h_hbm, u_hbm, o_hbm, h_v, u_v, ht_v, o_v, isem, osem):
    def ins(e):
        return (pltpu.make_async_copy(h_hbm.at[e], h_v.at[e], isem.at[e, 0]),
                pltpu.make_async_copy(u_hbm.at[e], u_v.at[e], isem.at[e, 1]))

    for e in range(E):
        for cpy in ins(e):
            cpy.start()

    def cols(i):
        return pl.ds(pl.multiple_of(lax.rem(i, 4) * 512, 512), 512)

    def outs(i, slot):
        return (pltpu.make_async_copy(o_v.at[slot], o_hbm.at[i // 4, :, cols(i)], osem.at[slot]),)

    def compute(i, slot):
        e = i // 4

        @pl.when(lax.rem(i, 4) == 0)
        def _():
            for cpy in ins(e):
                cpy.wait()
            ht_v[...] = h_v[e].T

        o_v[slot] = dot(ht_v[...], u_v[e, :, cols(i)]).astype(BF16)

    ring_loop(4 * E, RING, outs, compute)


def run_down(hs, us):
    anys = pl.BlockSpec(memory_space=pl.ANY)
    V = pltpu.VMEM
    return pl.pallas_call(
        down_kernel, name='moe_dw_down',
        in_specs=[anys, anys], out_specs=anys,
        out_shape=jax.ShapeDtypeStruct((E, F, D), BF16),
        scratch_shapes=[V((E, ROWS, F), BF16), V((E, ROWS, D), BF16), V((F, ROWS), BF16), V((RING, F, 512), BF16),
                        pltpu.SemaphoreType.DMA((E, 2)), pltpu.SemaphoreType.DMA((RING,))],
        compiler_params=pltpu.CompilerParams(vmem_limit_bytes=67043328),
        cost_estimate=pl.CostEstimate(flops=2 * E * ROWS * D * F, bytes_accessed=28_000_000, transcendentals=0),
    )(hs, us)


def exchange_pairs(kind):
    pairs = []
    for y in range(2):
        for x in range(2):
            for c in range(2):
                if (kind == 'prim') == (c == 0):
                    t = (y, 1 - x, c)
                else:
                    t = (1 - y, x, c)
                pairs.append((y * 4 + x * 2 + c, t[0] * 4 + t[1] * 2 + t[2]))
    return pairs


def solution(mesh):
    tok_spec = P(('dp', 'ei', 'eo'))
    exp_spec = P(('ei', 'eo'))

    def device_step(tok, idx, gate, wg, wu, wd, dy):
        _, _, c = place()
        pad = jnp.full((2, TD), -1.0, F32)
        half = jnp.concatenate([idx.T.astype(F32), pad, gate.T, pad], axis=0)
        zero = jnp.zeros_like(half)
        tbl = jnp.where(c == 0, jnp.concatenate([half, zero], axis=1), jnp.concatenate([zero, half], axis=1))

        layer_out, dgt, s1, k1, xs, us, hs, dgu = run_main(tok, dy, tbl, wg, wu, wd)
        perm = functools.partial(lax.ppermute, axis_name=('ei', 'eo'))
        r1 = perm(s1, perm=exchange_pairs('prim'))
        g_gate, g_up = run_gate_up(xs, dgu)
        g_down = run_down(hs, us)
        t = k1 + r1
        r2 = perm(t[1], perm=exchange_pairs('sec'))
        grad_tok = (t[0] + r2).astype(BF16)
        dgk = lax.dynamic_slice_in_dim(dgt[:K], c * TD, TD, axis=1).T
        return layer_out, grad_tok, dgk, g_gate, g_up, g_down

    return jax.shard_map(device_step, mesh=mesh,
                         in_specs=(tok_spec, tok_spec, tok_spec, exp_spec, exp_spec, exp_spec, tok_spec),
                         out_specs=(tok_spec, tok_spec, tok_spec, tok_spec, tok_spec, tok_spec), check_vma=False)
```

profile of v0, /device:TPU:0, one launch (start us, length us, event | category | flops | bytes accessed | tf_op | source)
XLA Modules:
  0.0 123.7 jit_solution(6805687418664089903)
XLA Ops:
  0.6 0.7 convert_bitcast_fusion
  1.3 0.7 pad_maximum_fusion
  2.0 0.7 pad_select_fusion.tbl_hbm
  2.7 79.9 %moe_main.1 = (bf16[64,2048]{1,0:T(8,128)(2,1)}, f32[8,128]{1,0:T(8,128)}, f32[2,64,2048]{2,1,0:T(8,128)}, f32[2,64,2048]{2,1,0:T(8,128)}, bf16[4,192,2048]{2,1,...) custom-call(bf16[64,2048]{1,0:T(8,128)(2,1)} %x_hbm.1, ...), custom_call_target="tpu_custom_call" | custom-call | flops 26575110144 | bytes 120000000 | tf_op jit(solution)/shard_map/moe_main/pallas_call | solution.py:401
  82.6 0.6 collective-permute-start
  83.2 18.4 %moe_dw_gate_up.1 = (bf16[4,2048,1408]{2,1,0:T(8,128)(2,1)}, bf16[4,2048,1408]{2,1,0:T(8,128)(2,1)}) custom-call(bf16[4,192,2048]{2,1,0:T(8,128)(2,1)} %get-tuple-element.20.x_hbm, bf16[4,192,2816]{2,1,0:T(8,128)(2,1)} %get-tuple-element.21.g_hbm), custom_call_target="tpu_custom_call" | custom-call | flops 8858370048 | bytes 55000000 | tf_op jit(solution)/shard_map/moe_dw_gate_up/pallas_call | solution.py:484
  101.5 0.0 collective-permute-done
  101.6 1.7 %add.18 = f32[2,64,2048]{2,1,0:T(8,128)S(1)} add(f32[2,64,2048]{2,1,0:T(8,128)} %get-tuple-element.17, f32[2,64,2048]{2,1,0:T(8,128)} %collective-permute-done) | non-fusion elementwise | flops 262144 | bytes 3145728 | tf_op jit(solution)/shard_map/add | solution.py:568
  103.2 0.0 copy-start
  103.2 1.0 copy-done
  104.2 0.9 slice_bitcast_fusion
  105.1 1.5 %collective-permute-start.1 = (f32[64,2048]{1,0:T(8,128)}, f32[64,2048]{1,0:T(8,128)}, u32[]{:S(2)}, u32[]{:S(2)}) collective-permute-start(f32[64,2048]{1,0:T(8,128)} %slice_bitcast_fusion), channel_id=1, source_target_pairs={{0,4},{1,3},{2,6},{3,1},{4,0},{5,7},{6,2},{7,5}} | collective-permute-start | bytes 1572872 | tf_op jit(solution)/shard_map/ppermute | solution.py:569
  106.6 1.3 %dynamic-slice_bitcast_fusion = f32[64,6]{0,1:T(8,128)} fusion(f32[6,128]{1,0:T(8,128)} %bitcast.15, s32[]{:T(128)S(6)} %select_n.21), kind=kLoop, calls=%fused_computation.6 | loop fusion | bytes 3076 | tf_op jit(solution)/shard_map/transpose | solution.py:571
  107.9 12.1 %moe_dw_down.1 = bf16[4,1408,2048]{2,1,0:T(8,128)(2,1)} custom-call(bf16[4,192,1408]{2,1,0:T(8,128)(2,1)} %get-tuple-element.24.h_hbm, bf16[4,192,2048]{2,1,0:T(8,128)(2,1)} %get-tuple-element.25.u_hbm), custom_call_target="tpu_custom_call" | custom-call | flops 4429185024 | bytes 28000000 | tf_op jit(solution)/shard_map/moe_dw_down/pallas_call | solution.py:528
  120.0 0.0 collective-permute-done.1
  120.0 2.0 %fusion.1 = bf16[64,2048]{1,0:T(8,128)(2,1)} fusion(f32[64,2048]{1,0:T(8,128)} %collective-permute-done.1, f32[2,64,2048]{2,1,0:T(8,128)} %copy-done), kind=kLoop, calls=%fused_computation.3 | loop fusion | flops 262144 | bytes 1310720 | tf_op jit(solution)/shard_map/convert_element_type | solution.py:570
  122.0 1.7 %copy.14 = bf16[64,2048]{1,0:T(8,128)(2,1)} copy(bf16[64,2048]{1,0:T(8,128)(2,1)} %get-tuple-element.32) | data formatting | bytes 524288
  (1 shorter events, 0.0 us)
Async XLA Ops:
  82.6 18.9 %collective-permute-start = (f32[2,64,2048]{2,1,0:T(8,128)}, f32[2,64,2048]{2,1,0:T(8,128)}, u32[]{:S(2)}, u32[]{:S(2)}) collective-permute-start(f32[2,64,2048]{2,1,0:T(8,128)} %get-tuple-element.18), channel_id=1, source_target_pairs={{0,2},{1,5},{2,0},{3,7},{4,6},{5,1},{6,4},{7,3}} | collective-permute-start | bytes 3145736 | tf_op jit(solution)/shard_map/ppermute | solution.py:565
  103.2 1.0 copy-start
  105.1 14.9 %collective-permute-start.1 = (f32[64,2048]{1,0:T(8,128)}, f32[64,2048]{1,0:T(8,128)}, u32[]{:S(2)}, u32[]{:S(2)}) collective-permute-start(f32[64,2048]{1,0:T(8,128)} %slice_bitcast_fusion), channel_id=1, source_target_pairs={{0,4},{1,3},{2,6},{3,1},{4,0},{5,7},{6,2},{7,5}} | collective-permute-start | bytes 1572872 | tf_op jit(solution)/shard_map/ppermute | solution.py:569
where the time goes:
time: 124 us
  Pallas kernels  110 us (89%)
  other arithmetic  5.67 us (5%)
  local copies, waits for them, and re-layouts  4.88 us (4%)
  starting transfers between devices  2.03 us (2%)
    pallas_call x1, Pallas kernels, run_main(): pl.pallas_call(main_kernel, name='moe_main', out_shape=(jax.ShapeDtypeStr...  79.9 us
    pallas_call x1, Pallas kernels, run_gate_up(): pl.pallas_call(gate_up_kernel, name='moe_dw_gate_up', in_specs=[anys, any...  18.4 us
    pallas_call x1, Pallas kernels, run_down(): pl.pallas_call(down_kernel, name='moe_dw_down', in_specs=[anys, anys], ou...  12.1 us
    unnamed x3, local copies, waits for them, and re-layouts  2.67 us
  transfers between devices with their start and end apart: 2, of which 0 were waited for; matrix products, arithmetic and copies ran while one was open for 1% of the time, Pallas kernels for 25%

commit v1 on v0

--- a/solution.py
+++ b/solution.py
@@ -43,9 +43,9 @@
     return v + f - 2 * v * f
 
 
-def main_kernel(x_hbm, dy_hbm, tbl_hbm, wg_hbm, wu_hbm, wd_hbm,
-                y_out, dgt_out, s1_out, k1_out, xs_out, us_out, hs_out, dgu_out,
-                wgu, wd, xall, dyall, tall, rk, gt, ab, oall, py, rb0, rb1, rb2,
+def main_kernel(x_hbm, dy_hbm, id_hbm, ga_hbm, wg_hbm, wu_hbm, wd_hbm,
+                y_out, dgt_out, s1_out, own_out, sec_out, xs_out, us_out, hs_out, dgu_out,
+                wgu, wd, xall, dyall, idall, gaall, rk, gt, psel, ab, oall, py, rb0, rb1, rb2,
                 dgs, dgr, xsb, usb, hsb, dgb,
                 wsem, lsem, snd, rcv, rs_s, rs_r, dg_s, dg_r, osem, psem, credit):
     dp = lax.axis_index('dp')
@@ -73,13 +73,10 @@
                 load(wu_hbm.at[e], wgu.at[sl, :, pl.ds(F, F)], wsem.at[sl, 1]),
                 load(wd_hbm.at[e], wd.at[sl], wsem.at[sl, 2]))
 
-    ins = (load(x_hbm, xall.at[me], lsem.at[0]), load(tbl_hbm, tall.at[me], lsem.at[1]),
-           load(dy_hbm, dyall.at[me], lsem.at[2]))
+    ins = (load(id_hbm, idall.at[me], lsem.at[0]), load(ga_hbm, gaall.at[me], lsem.at[1]),
+           load(x_hbm, xall.at[me], lsem.at[2]), load(dy_hbm, dyall.at[me], lsem.at[3]))
     for cpy in ins:
         cpy.start()
-    for e in range(2):
-        for cpy in weight_copies(e, e):
-            cpy.start()
 
     barrier = pltpu.get_barrier_semaphore()
     others = [lax.rem(me + k, ND) for k in range(1, ND)]
@@ -87,12 +84,15 @@
         pl.semaphore_signal(barrier, inc=1, device_id=(dp, t // 4, lax.rem(t, 4)), device_id_type=MESH)
     pl.semaphore_wait(barrier, ND - 1)
 
-    bufs = (xall, tall, dyall)
+    hw = D // 2
+    bufs = (lambda k: idall.at[k], lambda k: gaall.at[k],
+            lambda k: xall.at[k, :, pl.ds(0, hw)], lambda k: xall.at[k, :, pl.ds(hw, hw)],
+            lambda k: dyall.at[k])
     me_p, me_s, me_d = cp * 2 + c, cs * 2 + c, cd * 2 + c
 
     def ag_send(st, chunk, k, r, target):
         buf = bufs[st]
-        return rcopy(buf.at[chunk], buf.at[chunk], snd.at[st, k], rcv.at[st, r], target)
+        return rcopy(buf(chunk), buf(chunk), snd.at[st, k], rcv.at[st, r], target)
 
     def ag_wait(st, chunk, r):
         ag_send(st, chunk, 0, r, partner).wait_recv()
@@ -107,9 +107,11 @@
         ag_send(st, me_p, 3, 2, sec).start()
         ag_send(st, me_p, 4, 5, partner).start()
 
-    def ag_rest(st):
+    def ag_second(st):
         ag_wait(st, me_s, 1)
         ag_send(st, me_s, 5, 4, partner).start()
+
+    def ag_diag(st):
         ag_wait(st, me_d, 2)
         ag_send(st, me_d, 6, 6, partner).start()
 
@@ -125,31 +127,44 @@
                                              (me_p, partner), (me_s, partner), (me_d, partner))):
             ag_send(st, chunk, k, 0, target).wait_send()
 
-    ins[1].wait()
-    ag_open(1)
-    ins[0].wait()
-    ag_open(0)
+    for st in range(2):
+        ins[st].wait()
+        ag_open(st)
     ins[2].wait()
-    ag_first(1)
-    ag_rest(1)
-    ag_first(0)
+    ag_open(2)
+    ag_open(3)
+    ins[3].wait()
+    for cpy in weight_copies(0, 0):
+        cpy.start()
+    for step in (ag_first, ag_second, ag_diag):
+        for st in range(2):
+            step(st)
+    ag_first(2)
+    ag_second(2)
+    ag_first(3)
+    ag_second(3)
+    ag_last(0)
     ag_last(1)
 
     li = lax.broadcasted_iota(jnp.int32, (128, 128), 0)
     lj = lax.broadcasted_iota(jnp.int32, (128, 128), 1)
     upper = jnp.where((li // TD == lj // TD) & (li < lj), 1.0, 0.0).astype(BF16)
+    krow = lax.broadcasted_iota(jnp.int32, (2 * E * CAP, 128), 0).astype(F32)
+    pbase = (lax.broadcasted_iota(jnp.int32, (1, 128), 1) // TD * (E * CAP)).astype(F32)
     for p in range(4):
-        tb = tall[2 * p] + tall[2 * p + 1]
-        ids, gv = tb[0:8], tb[8:16]
+        ids = jnp.concatenate([idall[2 * p], idall[2 * p + 1]], axis=1)
+        gv = jnp.concatenate([gaall[2 * p], gaall[2 * p + 1]], axis=1)
+        sel = jnp.zeros((2 * E * CAP, 128), F32)
         for e in range(E):
-            eid = (me * E + e).astype(F32)
-            eq = ids == eid
+            eq = ids == me * E + e
             hit = jnp.sum(jnp.where(eq, 1.0, 0.0), axis=0, keepdims=True)
             gate = jnp.sum(jnp.where(eq, gv, 0.0), axis=0, keepdims=True)
             hit8 = jnp.broadcast_to(hit, (8, 128))
-            rank = dot(hit8.astype(BF16), upper)
-            rk[e, :, 128 * p:128 * (p + 1)] = jnp.where(hit8 > 0.5, rank, -1000.0)
+            rank = jnp.where(hit8 > 0.5, dot(hit8.astype(BF16), upper), -1000.0)
+            rk[e, :, 128 * p:128 * (p + 1)] = rank
             gt[e, :, 128 * p:128 * (p + 1)] = jnp.broadcast_to(gate, (8, 128))
+            sel = jnp.where(rank[0:1, :] + pbase + float(e * CAP) == krow, 1.0, sel)
+        psel[p] = sel.astype(BF16)
 
     tok = lax.broadcasted_iota(jnp.int32, (1, ND * TD), 1)
     slot_base = (tok // TD * CAP).astype(F32)
@@ -162,9 +177,13 @@
         for s in range(ND):
             oall[s, e, :, c0:c0 + width] = val[s * CAP:(s + 1) * CAP]
 
-    ag_rest(0)
-    ag_open(2)
-    ag_last(0)
+    ag_diag(2)
+    ag_diag(3)
+    for cpy in weight_copies(1, 1):
+        cpy.start()
+    ag_open(4)
+    ag_last(2)
+    ag_last(3)
 
     def fwd(e, carry):
         sl = lax.rem(e, 2)
@@ -210,59 +229,63 @@
 
         @pl.when(e == 1)
         def _():
-            ag_first(2)
+            ag_first(4)
 
         @pl.when(e == 2)
         def _():
-            ag_rest(2)
+            ag_second(4)
+            ag_diag(4)
 
         return carry
 
     lax.fori_loop(0, E, fwd, 0)
     load(xsb, xs_out.at[E - 1], osem.at[0]).wait()
     load(hsb, hs_out.at[E - 1], osem.at[1]).wait()
-    ag_last(2)
-
-    krow = lax.broadcasted_iota(jnp.int32, (2 * E * CAP, 128), 0).astype(F32)
-    ptok = lax.broadcasted_iota(jnp.int32, (1, 128), 1)
-    pbase = (ptok // TD * (E * CAP)).astype(F32)
-
-    def scatter(gated, put):
-        def body(p, carry):
-            sel = jnp.zeros((2 * E * CAP, 128), F32)
-            lanes = pl.ds(pl.multiple_of(p * 128, 128), 128)
-            for e in range(E):
-                m = (rk[e, :, lanes][0:1, :] + pbase + float(e * CAP)) == krow
-                sel = jnp.where(m, gt[e, :, lanes][0:1, :] if gated else 1.0, sel)
-            if gated:
-                g1 = sel.astype(BF16)
-                r1 = sel - g1.astype(F32)
-                g2 = r1.astype(BF16)
-                g3 = (r1 - g2.astype(F32)).astype(BF16)
-                lhs = jnp.concatenate([g1, g2, g3], axis=1)
-            else:
-                lhs = sel.astype(BF16)
-            for n in range(4):
-                rhs = oall[pl.ds(2 * p, 2), :, :, 512 * n:512 * (n + 1)].reshape(2 * E * CAP, 512)
-                r = dot(lhs, rhs, TN)
-                if gated:
-                    r = r[0:128] + (r[128:256] + r[256:384])
-                put(p, slice(512 * n, 512 * (n + 1)), r)
-            return carry
-
-        lax.fori_loop(0, 4, body, 0)
-
-    def put_y(p, cols, r):
-        py[0, p, :, cols] = r[0:TD]
-        py[1, p, :, cols] = r[TD:]
-
-    scatter(True, put_y)
+    ag_last(4)
+
+    def combine_y(p, carry):
+        lanes = pl.ds(pl.multiple_of(p * 128, 128), 128)
+        gates = jnp.zeros((2 * E * CAP, 128), F32)
+        for e in range(E):
+            hit = rk[e, :, lanes][0:1, :] + pbase + float(e * CAP) == krow
+            gates = jnp.where(hit, gt[e, :, lanes][0:1, :], gates)
+        g1 = gates.astype(BF16)
+        rest = gates - g1.astype(F32)
+        g2 = rest.astype(BF16)
+        g3 = (rest - g2.astype(F32)).astype(BF16)
+        lhs = jnp.concatenate([g1, g2, g3], axis=1)
+        for n in range(4):
+            cols = slice(512 * n, 512 * (n + 1))
+            rhs = oall[pl.ds(2 * p, 2), :, :, cols].reshape(2 * E * CAP, 512)
+            r = dot(lhs, rhs, TN)
+            r = r[0:128] + (r[128:256] + r[256:384])
+            py[0, p, :, cols] = r[0:TD]
+            py[1, p, :, cols] = r[TD:]
+        return carry
+
+    lax.fori_loop(0, 4, combine_y, 0)
 
     rs0 = rcopy(py.at[1 - c], rb0, rs_s.at[0], rs_r.at[0], partner)
     rs1a = rcopy(py.at[c, cd], rb1.at[1], rs_s.at[1], rs_r.at[1], prim)
     rs1b = rcopy(py.at[c, cp], rb1.at[0], rs_s.at[2], rs_r.at[2], prim)
     rs2 = rcopy(py.at[c, cs], rb2, rs_s.at[3], rs_r.at[3], sec)
     rs0.start()
+
+    def dx_copy(m):
+        cols = pl.ds(512 * m, 512)
+        return rcopy(ab.at[:, pl.ds(pl.multiple_of((1 - c) * TD, TD), TD), cols], rb0.at[:, :, cols],
+                     rs_s.at[4 + m], rs_r.at[4 + m], partner)
+
+    def combine_dx(m):
+        cols = slice(512 * m, 512 * (m + 1))
+
+        def body(p, carry):
+            rhs = oall[pl.ds(2 * p, 2), :, :, cols].reshape(2 * E * CAP, 512)
+            ab[p, 0:2 * TD, cols] = dot(psel[p], rhs, TN)
+            return carry
+
+        lax.fori_loop(0, 4, body, 0)
+        dx_copy(m).start()
 
     def bwd(n, carry):
         e = E - 1 - n
@@ -320,6 +343,12 @@
             dxt = dot(wgu[sl, 512 * m:512 * (m + 1), :], dgb[...], NT)
             put_rows(e, 512 * m, 512, dxt.T.astype(BF16))
 
+            @pl.when(n == E - 1)
+            def _():
+                if m == 0:
+                    pl.semaphore_wait(credit, 1)
+                combine_dx(m)
+
         @pl.when(n < 2)
         def _():
             for cpy in weight_copies(1 - n, sl)[:2]:
@@ -348,43 +377,39 @@
         sends.append(cpy)
     dgr[me] = dgs[:, :, pl.ds(pl.multiple_of(chip * 128, 128), 128)]
 
-    def put_dx(p, cols, r):
-        ab[p, 0:2 * TD, cols] = r
-
-    scatter(False, put_dx)
-    pl.semaphore_wait(credit, 1)
-    dx0 = rcopy(ab.at[:, pl.ds(pl.multiple_of((1 - c) * TD, TD), TD), pl.ds(0, D)], rb0,
-                rs_s.at[4], rs_r.at[4], partner)
-    dx0.start()
-
     rs1b.wait_recv()
     rs2.wait_recv()
     y_out[...] = (py[c, chip] + rb1[0] + rb2[...]).astype(BF16)
 
+    own_rows = pl.ds(pl.multiple_of(c * TD, TD), TD)
+    dst = ((cp, s1_out.at[0]), (cd, s1_out.at[1]), (chip, own_out), (cs, sec_out))
+    parts = []
+    for m in range(4):
+        dx_copy(m).wait_recv()
+        for i, (k, out) in enumerate(dst):
+            cols = slice(512 * m, 512 * (m + 1))
+            ab[i, 2 * TD:3 * TD, cols] = ab[k, own_rows, cols] + rb0[k, :, cols]
+            cpy = load(ab.at[i, pl.ds(2 * TD, TD), pl.ds(512 * m, 512)], out.at[:, pl.ds(512 * m, 512)], psem.at[i, m])
+            cpy.start()
+            parts.append(cpy)
+
     for i, t in enumerate(others):
         rcopy(dgs.at[:, :, pl.ds(0, 128)], dgr.at[t], dg_s.at[i], dg_r.at[t], partner).wait_recv()
-    tb = tall[2 * chip] + tall[2 * chip + 1]
-    ids = tb[0:8]
-    acc = jnp.zeros((8, 128), F32)
+    ids = idall[me]
+    acc = jnp.zeros((K, TD), F32)
     for t in range(ND):
         for e in range(E):
-            acc = acc + jnp.where(ids == float(t * E + e), dgr[t, e], 0.0)
+            row = dgr[t, e][0:1, :]
+            row = jnp.where(c == 0, row[:, 0:TD], row[:, TD:2 * TD])
+            acc = acc + jnp.where(ids == t * E + e, row, 0.0)
     dgt_out[...] = acc
 
-    dx0.wait_recv()
-    own_rows = pl.ds(pl.multiple_of(c * TD, TD), TD)
-    parts = []
-    for i, (k, out) in enumerate(((cp, s1_out.at[0]), (cd, s1_out.at[1]), (chip, k1_out.at[0]), (cs, k1_out.at[1]))):
-        ab[i, 2 * TD:3 * TD, 0:D] = ab[k, own_rows, 0:D] + rb0[k]
-        cpy = load(ab.at[i, pl.ds(2 * TD, TD), pl.ds(0, D)], out, psem.at[i])
-        cpy.start()
-        parts.append(cpy)
-
-    dx0.wait_send()
+    for m in range(4):
+        dx_copy(m).wait_send()
     rs1a.wait_send()
     rs1b.wait_send()
     rs2.wait_send()
-    for st in range(3):
+    for st in range(5):
         ag_sent(st)
     for cpy in sends:
         cpy.wait_send()
@@ -392,7 +417,7 @@
         cpy.wait()
 
 
-def run_main(tok, dy, tbl, wg, wu, wd):
+def run_main(tok, dy, idt, gat, wg, wu, wd):
     anys = pl.BlockSpec(memory_space=pl.ANY)
     vm = pl.BlockSpec(memory_space=pltpu.VMEM)
     V = pltpu.VMEM
@@ -401,27 +426,28 @@
     return pl.pallas_call(
         main_kernel,
         name='moe_main',
-        out_shape=(jax.ShapeDtypeStruct((TD, D), BF16), jax.ShapeDtypeStruct((8, 128), F32),
-                   jax.ShapeDtypeStruct((2, TD, D), F32), jax.ShapeDtypeStruct((2, TD, D), F32),
+        out_shape=(jax.ShapeDtypeStruct((TD, D), BF16), jax.ShapeDtypeStruct((K, TD), F32),
+                   jax.ShapeDtypeStruct((2, TD, D), F32), jax.ShapeDtypeStruct((TD, D), F32),
+                   jax.ShapeDtypeStruct((TD, D), F32),
                    jax.ShapeDtypeStruct((E, ROWS, D), BF16), jax.ShapeDtypeStruct((E, ROWS, D), BF16),
                    jax.ShapeDtypeStruct((E, ROWS, F), BF16), jax.ShapeDtypeStruct((E, ROWS, 2 * F), BF16)),
-        in_specs=[anys] * 6,
-        out_specs=(vm, vm) + (anys,) * 6,
+        in_specs=[anys] * 7,
+        out_specs=(vm, vm) + (anys,) * 7,
         scratch_shapes=[
             V((2, D, 2 * F), BF16), V((2, F, D), BF16),
-            V((ND, TD, D), BF16), V((ND, TD, D), BF16), V((ND, 16, 128), F32),
-            V((E, 8, ND * TD), F32), V((E, 8, ND * TD), F32),
+            V((ND, TD, D), BF16), V((ND, TD, D), BF16), V((ND, K, TD), jnp.int32), V((ND, K, TD), F32),
+            V((E, 8, ND * TD), F32), V((E, 8, ND * TD), F32), V((4, 2 * E * CAP, 128), BF16),
             V((E, ROWS, 2 * F), F32), V((ND, E, CAP, D), BF16),
             V((2, 4, TD, D), F32), V((4, TD, D), F32), V((2, TD, D), F32), V((TD, D), F32),
             V((E, 8, ND * TD), F32), V((ND, E, 8, 128), F32),
             V((ROWS, D), BF16), V((ROWS, D), BF16), V((ROWS, F), BF16), V((ROWS, 2 * F), BF16),
-            S((2, 3)), S((3,)), S((3, 7)), S((3, 7)), S((5,)), S((5,)), S((7,)), S((ND,)), S((2,)), S((4,)),
+            S((2, 3)), S((4,)), S((5, 7)), S((5, 7)), S((8,)), S((8,)), S((7,)), S((ND,)), S((2,)), S((4, 4)),
             pltpu.SemaphoreType.REGULAR,
         ],
         compiler_params=pltpu.CompilerParams(collective_id=0, has_side_effects=True,
                                              vmem_limit_bytes=67043328),
         cost_estimate=pl.CostEstimate(flops=flops, bytes_accessed=120_000_000, transcendentals=0),
-    )(tok, dy, tbl, wg, wu, wd)
+    )(tok, dy, idt, gat, wg, wu, wd)
 
 
 RING = 4
@@ -554,21 +580,14 @@
     exp_spec = P(('ei', 'eo'))
 
     def device_step(tok, idx, gate, wg, wu, wd, dy):
-        _, _, c = place()
-        pad = jnp.full((2, TD), -1.0, F32)
-        half = jnp.concatenate([idx.T.astype(F32), pad, gate.T, pad], axis=0)
-        zero = jnp.zeros_like(half)
-        tbl = jnp.where(c == 0, jnp.concatenate([half, zero], axis=1), jnp.concatenate([zero, half], axis=1))
-
-        layer_out, dgt, s1, k1, xs, us, hs, dgu = run_main(tok, dy, tbl, wg, wu, wd)
+        layer_out, dgt, s1, own, second, xs, us, hs, dgu = run_main(tok, dy, idx.T, gate.T, wg, wu, wd)
         perm = functools.partial(lax.ppermute, axis_name=('ei', 'eo'))
         r1 = perm(s1, perm=exchange_pairs('prim'))
         g_gate, g_up = run_gate_up(xs, dgu)
         g_down = run_down(hs, us)
-        t = k1 + r1
-        r2 = perm(t[1], perm=exchange_pairs('sec'))
-        grad_tok = (t[0] + r2).astype(BF16)
-        dgk = lax.dynamic_slice_in_dim(dgt[:K], c * TD, TD, axis=1).T
+        r2 = perm(second + r1[1], perm=exchange_pairs('sec'))
+        grad_tok = (own + r1[0] + r2).astype(BF16)
+        dgk = dgt.T
         return layer_out, grad_tok, dgk, g_gate, g_up, g_down
 
     return jax.shard_map(device_step, mesh=mesh,

time: 124 us -> 137 us (1.10)
  waiting for transfers between devices: 0.01 us -> 13.4 us
  Pallas kernels: 110 us -> 112 us
  other arithmetic: 5.67 us -> 4.05 us
    ppermute x1, waiting for transfers between devices: 0.01 us -> 13.4 us  [device_step(): r1 = perm(s1, perm=exchange_pairs('prim'))]
    pallas_call x1, Pallas kernels: 79.9 us -> 81.8 us  [run_main(): pl.pallas_call(main_kernel, name='moe_main', out_shape=(jax.ShapeDtypeStr...]
    unnamed x3 -> x4, local copies, waits for them, and re-layouts: 2.67 us -> 3.98 us
  transfers between devices with their start and end apart: 2 -> 2, of which waited for: 0 -> 1; matrix products, arithmetic and copies ran while one was open for 1% -> 0% of each run, Pallas kernels for 25% -> 22%
where the time goes in v1:
time: 137 us
  Pallas kernels  112 us (82%)
  waiting for transfers between devices  13.4 us (10%)
  other arithmetic  4.05 us (3%)
  local copies, waits for them, and re-layouts  3.98 us (3%)
  starting transfers between devices  2.72 us (2%)
    pallas_call x1, Pallas kernels, run_main(): pl.pallas_call(main_kernel, name='moe_main', out_shape=(jax.ShapeDtypeStr...  81.8 us
    pallas_call x1, Pallas kernels, run_gate_up(): pl.pallas_call(gate_up_kernel, name='moe_dw_gate_up', in_specs=[anys, any...  18.4 us
    ppermute x1, waiting for transfers between devices, device_step(): r1 = perm(s1, perm=exchange_pairs('prim'))  13.4 us
    pallas_call x1, Pallas kernels, run_down(): pl.pallas_call(down_kernel, name='moe_dw_down', in_specs=[anys, anys], ou...  12.1 us
    unnamed x4, local copies, waits for them, and re-layouts  3.98 us
  transfers between devices with their start and end apart: 2, of which 1 were waited for; matrix products, arithmetic and copies ran while one was open for 0% of the time, Pallas kernels for 22%

profile of v1, /device:TPU:0, one launch (start us, length us, event | category | flops | bytes accessed | tf_op | source)
XLA Modules:
  0.0 137.1 jit_solution(5116045368611242336)
XLA Ops:
  0.6 81.8 %moe_main.1 = (bf16[64,2048]{1,0:T(8,128)(2,1)}, f32[6,64]{1,0:T(8,128)}, f32[2,64,2048]{2,1,0:T(8,128)}, f32[64,2048]{1,0:T(8,128)}, f32[64,2048]{1,0:T(8,128)}...) custom-call(bf16[64,2048]{1,0:T(8,128)(2,1)} %x_hbm.1, ...), custom_call_target="tpu_custom_call" | custom-call | flops 26575110144 | bytes 120000000 | tf_op jit(solution)/shard_map/moe_main/pallas_call | solution.py:426
  82.4 1.6 %collective-permute-start = (f32[2,64,2048]{2,1,0:T(8,128)}, f32[2,64,2048]{2,1,0:T(8,128)S(1)}, u32[]{:S(2)}, u32[]{:S(2)}) collective-permute-start(f32[2,64,2048]{2,1,0:T(8,128)} %get-tuple-element.19), channel_id=1, source_target_pairs={{0,2},{1,5},{2,0},{3,7},{4,6},{5,1},{6,4},{7,3}} | collective-permute-start | bytes 3145736 | tf_op jit(solution)/shard_map/ppermute | solution.py:585
  84.1 13.4 %collective-permute-done = f32[2,64,2048]{2,1,0:T(8,128)S(1)} collective-permute-done((f32[2,64,2048]{2,1,0:T(8,128)}, f32[2,64,2048]{2,1,0:T(8,128)S(1)}, u32[]{:S(2)}, u32[]{:S(2)}) %collective-permute-start) | collective-permute-done | bytes 1048608 | tf_op jit(solution)/shard_map/ppermute | solution.py:585
  97.5 0.0 copy-start
  97.5 1.0 copy-done
  98.5 1.9 %fusion = f32[64,2048]{1,0:T(8,128)} fusion(f32[64,2048]{1,0:T(8,128)} %get-tuple-element.20, f32[2,64,2048]{2,1,0:T(8,128)S(1)} %collective-permute-done), kind=kLoop, calls=%fused_computation.1 | loop fusion | flops 131072 | bytes 1572864 | tf_op jit(solution)/shard_map/add | solution.py:588
  100.4 1.1 collective-permute-start.1
  101.5 18.4 %moe_dw_gate_up.1 = (bf16[4,2048,1408]{2,1,0:T(8,128)(2,1)}, bf16[4,2048,1408]{2,1,0:T(8,128)(2,1)}) custom-call(bf16[4,192,2048]{2,1,0:T(8,128)(2,1)} %get-tuple-element.22.x_hbm, bf16[4,192,2816]{2,1,0:T(8,128)(2,1)} %get-tuple-element.23.g_hbm), custom_call_target="tpu_custom_call" | custom-call | flops 8858370048 | bytes 55000000 | tf_op jit(solution)/shard_map/moe_dw_gate_up/pallas_call | solution.py:510
  119.9 12.1 %moe_dw_down.1 = bf16[4,1408,2048]{2,1,0:T(8,128)(2,1)} custom-call(bf16[4,192,1408]{2,1,0:T(8,128)(2,1)} %get-tuple-element.26.h_hbm, bf16[4,192,2048]{2,1,0:T(8,128)(2,1)} %get-tuple-element.27.u_hbm), custom_call_target="tpu_custom_call" | custom-call | flops 4429185024 | bytes 28000000 | tf_op jit(solution)/shard_map/moe_dw_down/pallas_call | solution.py:554
  132.0 0.0 collective-permute-done.1
  132.0 2.1 %fusion.3 = bf16[64,2048]{1,0:T(8,128)(2,1)} fusion(f32[64,2048]{1,0:T(8,128)} %collective-permute-done.1, f32[64,2048]{1,0:T(8,128)} %get-tuple-element.18, f32[2,64,2048]{2,1,0:T(8,128)} %copy-done), kind=kLoop, calls=%fused_computation.5 | loop fusion | flops 393216 | bytes 1835008 | tf_op jit(solution)/shard_map/convert_element_type | solution.py:589
  134.2 1.7 %copy.15 = bf16[64,2048]{1,0:T(8,128)(2,1)} copy(bf16[64,2048]{1,0:T(8,128)(2,1)} %get-tuple-element.34) | data formatting | bytes 524288
  135.8 1.3 copy.16
Async XLA Ops:
  82.4 15.0 %collective-permute-start = (f32[2,64,2048]{2,1,0:T(8,128)}, f32[2,64,2048]{2,1,0:T(8,128)S(1)}, u32[]{:S(2)}, u32[]{:S(2)}) collective-permute-start(f32[2,64,2048]{2,1,0:T(8,128)} %get-tuple-element.19), channel_id=1, source_target_pairs={{0,2},{1,5},{2,0},{3,7},{4,6},{5,1},{6,4},{7,3}} | collective-permute-start | bytes 3145736 | tf_op jit(solution)/shard_map/ppermute | solution.py:585
  97.5 1.0 copy-start
  100.4 31.6 %collective-permute-start.1 = (f32[64,2048]{1,0:T(8,128)}, f32[64,2048]{1,0:T(8,128)}, u32[]{:S(2)}, u32[]{:S(2)}) collective-permute-start(f32[64,2048]{1,0:T(8,128)} %fusion), channel_id=1, source_target_pairs={{0,4},{1,3},{2,6},{3,1},{4,0},{5,7},{6,2},{7,5}} | collective-permute-start | bytes 1572872 | tf_op jit(solution)/shard_map/ppermute | solution.py:588

commit v2 on v1

--- a/solution.py
+++ b/solution.py
@@ -68,10 +68,23 @@
     def load(src, dst, sem):
         return pltpu.make_async_copy(src, dst, sem)
 
-    def weight_copies(e, sl):
-        return (load(wg_hbm.at[e], wgu.at[sl, :, pl.ds(0, F)], wsem.at[sl, 0]),
-                load(wu_hbm.at[e], wgu.at[sl, :, pl.ds(F, F)], wsem.at[sl, 1]),
-                load(wd_hbm.at[e], wd.at[sl], wsem.at[sl, 2]))
+    def start_gate_up(e, sl):
+        for lo in range(0, D, 256):
+            rows = pl.ds(lo, 256)
+            load(wg_hbm.at[e, rows], wgu.at[sl, rows, pl.ds(0, F)], wsem.at[sl, 0]).start()
+            load(wu_hbm.at[e, rows], wgu.at[sl, rows, pl.ds(F, F)], wsem.at[sl, 1]).start()
+
+    def start_down(e, sl):
+        for lo in range(0, F, 176):
+            rows = pl.ds(lo, 176)
+            load(wd_hbm.at[e, rows], wd.at[sl, rows], wsem.at[sl, 2]).start()
+
+    def wait_gate_up(e, sl):
+        load(wg_hbm.at[e], wgu.at[sl, :, pl.ds(0, F)], wsem.at[sl, 0]).wait()
+        load(wu_hbm.at[e], wgu.at[sl, :, pl.ds(F, F)], wsem.at[sl, 1]).wait()
+
+    def wait_down(e, sl):
+        load(wd_hbm.at[e], wd.at[sl], wsem.at[sl, 2]).wait()
 
     ins = (load(id_hbm, idall.at[me], lsem.at[0]), load(ga_hbm, gaall.at[me], lsem.at[1]),
            load(x_hbm, xall.at[me], lsem.at[2]), load(dy_hbm, dyall.at[me], lsem.at[3]))
@@ -134,8 +147,8 @@
     ag_open(2)
     ag_open(3)
     ins[3].wait()
-    for cpy in weight_copies(0, 0):
-        cpy.start()
+    start_gate_up(0, 0)
+    start_down(0, 0)
     for step in (ag_first, ag_second, ag_diag):
         for st in range(2):
             step(st)
@@ -179,8 +192,8 @@
 
     ag_diag(2)
     ag_diag(3)
-    for cpy in weight_copies(1, 1):
-        cpy.start()
+    start_gate_up(1, 1)
+    start_down(1, 1)
     ag_open(4)
     ag_last(2)
     ag_last(3)
@@ -197,9 +210,7 @@
         for n in range(4):
             xsb[:, 512 * n:512 * (n + 1)] = dot(sel, xall[:, :, 512 * n:512 * (n + 1)].reshape(ND * TD, 512)).astype(BF16)
         load(xsb, xs_out.at[e], osem.at[0]).start()
-        cg, cu, cw = weight_copies(e, sl)
-        cg.wait()
-        cu.wait()
+        wait_gate_up(e, sl)
         for n in range(6):
             lo, w = 256 * n, 256 if n < 5 else 128
             if w == 256:
@@ -216,16 +227,15 @@
 
         @pl.when(e < 2)
         def _():
-            for cpy in weight_copies(e + 2, sl)[:2]:
-                cpy.start()
-
-        cw.wait()
+            start_gate_up(e + 2, sl)
+
+        wait_down(e, sl)
         for n in range(8):
             put_rows(e, 256 * n, 256, dot(hsb[...], wd[sl, :, 256 * n:256 * (n + 1)]).astype(BF16))
 
         @pl.when(e < 2)
         def _():
-            weight_copies(e + 2, sl)[2].start()
+            start_down(e + 2, sl)
 
         @pl.when(e == 1)
         def _():
@@ -309,11 +319,10 @@
         dgrow = jnp.sum(jnp.where(mask, dgv, 0.0), axis=0, keepdims=True)
         dgs[e] = jnp.broadcast_to(dgrow, (8, ND * TD))
         load(usb, us_out.at[e], osem.at[0]).start()
-        cg, cu, cw = weight_copies(e, sl)
 
         @pl.when(n >= 2)
         def _():
-            cw.wait()
+            wait_down(e, sl)
 
         for lo, hi in ((0, 768), (768, F)):
             q = dot(wd[sl, lo:hi, :], usb[...], NT).T
@@ -326,7 +335,7 @@
 
         @pl.when(n < 2)
         def _():
-            weight_copies(1 - n, sl)[2].start()
+            start_down(1 - n, sl)
 
         @pl.when(n == 2)
         def _():
@@ -336,8 +345,7 @@
 
         @pl.when(n >= 2)
         def _():
-            cg.wait()
-            cu.wait()
+            wait_gate_up(e, sl)
 
         for m in range(4):
             dxt = dot(wgu[sl, 512 * m:512 * (m + 1), :], dgb[...], NT)
@@ -351,8 +359,7 @@
 
         @pl.when(n < 2)
         def _():
-            for cpy in weight_copies(1 - n, sl)[:2]:
-                cpy.start()
+            start_gate_up(1 - n, sl)
 
         @pl.when(n == 0)
         def _():

time: 137 us -> 137 us (level)
  no operation moved by 1% of the time
where the time goes in v2:
time: 137 us
  Pallas kernels  112 us (82%)
  waiting for transfers between devices  13.4 us (10%)
  other arithmetic  4.05 us (3%)
  local copies, waits for them, and re-layouts  3.98 us (3%)
  starting transfers between devices  2.73 us (2%)
    pallas_call x1, Pallas kernels, run_main(): pl.pallas_call(main_kernel, name='moe_main', out_shape=(jax.ShapeDtypeStr...  81.9 us
    pallas_call x1, Pallas kernels, run_gate_up(): pl.pallas_call(gate_up_kernel, name='moe_dw_gate_up', in_specs=[anys, any...  18.4 us
    ppermute x1, waiting for transfers between devices, device_step(): r1 = perm(s1, perm=exchange_pairs('prim'))  13.4 us
    pallas_call x1, Pallas kernels, run_down(): pl.pallas_call(down_kernel, name='moe_dw_down', in_specs=[anys, anys], ou...  12.1 us
    unnamed x4, local copies, waits for them, and re-layouts  3.98 us
  transfers between devices with their start and end apart: 2, of which 1 were waited for; matrix products, arithmetic and copies ran while one was open for 0% of the time, Pallas kernels for 22%

profile of v2, /device:TPU:0, one launch (start us, length us, event | category | flops | bytes accessed | tf_op | source)
XLA Modules:
  0.0 137.2 jit_solution(1108301278312816183)
XLA Ops:
  0.6 81.9 %moe_main.1 = (bf16[64,2048]{1,0:T(8,128)(2,1)}, f32[6,64]{1,0:T(8,128)}, f32[2,64,2048]{2,1,0:T(8,128)}, f32[64,2048]{1,0:T(8,128)}, f32[64,2048]{1,0:T(8,128)}...) custom-call(bf16[64,2048]{1,0:T(8,128)(2,1)} %x_hbm.1, ...), custom_call_target="tpu_custom_call" | custom-call | flops 26575110144 | bytes 120000000 | tf_op jit(solution)/shard_map/moe_main/pallas_call | solution.py:433
  82.5 1.7 %collective-permute-start = (f32[2,64,2048]{2,1,0:T(8,128)}, f32[2,64,2048]{2,1,0:T(8,128)S(1)}, u32[]{:S(2)}, u32[]{:S(2)}) collective-permute-start(f32[2,64,2048]{2,1,0:T(8,128)} %get-tuple-element.19), channel_id=1, source_target_pairs={{0,2},{1,5},{2,0},{3,7},{4,6},{5,1},{6,4},{7,3}} | collective-permute-start | bytes 3145736 | tf_op jit(solution)/shard_map/ppermute | solution.py:592
  84.2 13.4 %collective-permute-done = f32[2,64,2048]{2,1,0:T(8,128)S(1)} collective-permute-done((f32[2,64,2048]{2,1,0:T(8,128)}, f32[2,64,2048]{2,1,0:T(8,128)S(1)}, u32[]{:S(2)}, u32[]{:S(2)}) %collective-permute-start) | collective-permute-done | bytes 1048608 | tf_op jit(solution)/shard_map/ppermute | solution.py:592
  97.5 0.0 copy-start
  97.5 1.0 copy-done
  98.6 1.9 %fusion = f32[64,2048]{1,0:T(8,128)} fusion(f32[64,2048]{1,0:T(8,128)} %get-tuple-element.20, f32[2,64,2048]{2,1,0:T(8,128)S(1)} %collective-permute-done), kind=kLoop, calls=%fused_computation.1 | loop fusion | flops 131072 | bytes 1572864 | tf_op jit(solution)/shard_map/add | solution.py:595
  100.5 1.1 collective-permute-start.1
  101.6 18.4 %moe_dw_gate_up.1 = (bf16[4,2048,1408]{2,1,0:T(8,128)(2,1)}, bf16[4,2048,1408]{2,1,0:T(8,128)(2,1)}) custom-call(bf16[4,192,2048]{2,1,0:T(8,128)(2,1)} %get-tuple-element.22.x_hbm, bf16[4,192,2816]{2,1,0:T(8,128)(2,1)} %get-tuple-element.23.g_hbm), custom_call_target="tpu_custom_call" | custom-call | flops 8858370048 | bytes 55000000 | tf_op jit(solution)/shard_map/moe_dw_gate_up/pallas_call | solution.py:517
  120.0 12.1 %moe_dw_down.1 = bf16[4,1408,2048]{2,1,0:T(8,128)(2,1)} custom-call(bf16[4,192,1408]{2,1,0:T(8,128)(2,1)} %get-tuple-element.26.h_hbm, bf16[4,192,2048]{2,1,0:T(8,128)(2,1)} %get-tuple-element.27.u_hbm), custom_call_target="tpu_custom_call" | custom-call | flops 4429185024 | bytes 28000000 | tf_op jit(solution)/shard_map/moe_dw_down/pallas_call | solution.py:561
  132.1 0.0 collective-permute-done.1
  132.1 2.1 %fusion.3 = bf16[64,2048]{1,0:T(8,128)(2,1)} fusion(f32[64,2048]{1,0:T(8,128)} %collective-permute-done.1, f32[64,2048]{1,0:T(8,128)} %get-tuple-element.18, f32[2,64,2048]{2,1,0:T(8,128)} %copy-done), kind=kLoop, calls=%fused_computation.5 | loop fusion | flops 393216 | bytes 1835008 | tf_op jit(solution)/shard_map/convert_element_type | solution.py:596
  134.2 1.7 %copy.15 = bf16[64,2048]{1,0:T(8,128)(2,1)} copy(bf16[64,2048]{1,0:T(8,128)(2,1)} %get-tuple-element.34) | data formatting | bytes 524288
  135.9 1.3 copy.16
Async XLA Ops:
  82.5 15.0 %collective-permute-start = (f32[2,64,2048]{2,1,0:T(8,128)}, f32[2,64,2048]{2,1,0:T(8,128)S(1)}, u32[]{:S(2)}, u32[]{:S(2)}) collective-permute-start(f32[2,64,2048]{2,1,0:T(8,128)} %get-tuple-element.19), channel_id=1, source_target_pairs={{0,2},{1,5},{2,0},{3,7},{4,6},{5,1},{6,4},{7,3}} | collective-permute-start | bytes 3145736 | tf_op jit(solution)/shard_map/ppermute | solution.py:592
  97.5 1.0 copy-start
  100.5 31.6 %collective-permute-start.1 = (f32[64,2048]{1,0:T(8,128)}, f32[64,2048]{1,0:T(8,128)}, u32[]{:S(2)}, u32[]{:S(2)}) collective-permute-start(f32[64,2048]{1,0:T(8,128)} %fusion), channel_id=1, source_target_pairs={{0,4},{1,3},{2,6},{3,1},{4,0},{5,7},{6,2},{7,5}} | collective-permute-start | bytes 1572872 | tf_op jit(solution)/shard_map/ppermute | solution.py:595

commit v3 on v2

--- a/solution.py
+++ b/solution.py
@@ -97,9 +97,9 @@
         pl.semaphore_signal(barrier, inc=1, device_id=(dp, t // 4, lax.rem(t, 4)), device_id_type=MESH)
     pl.semaphore_wait(barrier, ND - 1)
 
-    hw = D // 2
+    hw = TD // 2
     bufs = (lambda k: idall.at[k], lambda k: gaall.at[k],
-            lambda k: xall.at[k, :, pl.ds(0, hw)], lambda k: xall.at[k, :, pl.ds(hw, hw)],
+            lambda k: xall.at[k, pl.ds(0, hw)], lambda k: xall.at[k, pl.ds(hw, hw)],
             lambda k: dyall.at[k])
     me_p, me_s, me_d = cp * 2 + c, cs * 2 + c, cd * 2 + c
 
@@ -324,7 +324,8 @@
         def _():
             wait_down(e, sl)
 
-        for lo, hi in ((0, 768), (768, F)):
+        for lo in range(0, F, 256):
+            hi = min(lo + 256, F)
             q = dot(wd[sl, lo:hi, :], usb[...], NT).T
             a = ab[e, :, lo:hi]
             b = ab[e, :, F + lo:F + hi]
@@ -351,12 +352,6 @@
             dxt = dot(wgu[sl, 512 * m:512 * (m + 1), :], dgb[...], NT)
             put_rows(e, 512 * m, 512, dxt.T.astype(BF16))
 
-            @pl.when(n == E - 1)
-            def _():
-                if m == 0:
-                    pl.semaphore_wait(credit, 1)
-                combine_dx(m)
-
         @pl.when(n < 2)
         def _():
             start_gate_up(1 - n, sl)
@@ -372,6 +367,9 @@
         return carry
 
     lax.fori_loop(0, E, bwd, 0)
+    pl.semaphore_wait(credit, 1)
+    for m in range(4):
+        combine_dx(m)
     load(usb, us_out.at[0], osem.at[0]).wait()
     load(dgb, dgu_out.at[0], osem.at[1]).wait()
 

time: 137 us -> 129 us (0.942)
  Pallas kernels: 112 us -> 104 us
    pallas_call x1, Pallas kernels: 81.9 us -> 73.4 us  [run_main(): pl.pallas_call(main_kernel, name='moe_main', out_shape=(jax.ShapeDtypeStr...]
  transfers between devices with their start and end apart: 2 -> 2, of which waited for: 1 -> 1; matrix products, arithmetic and copies ran while one was open for 0% -> 0% of each run, Pallas kernels for 22% -> 24%
where the time goes in v3:
time: 129 us
  Pallas kernels  104 us (81%)
  waiting for transfers between devices  13.4 us (10%)
  other arithmetic  4.05 us (3%)
  local copies, waits for them, and re-layouts  3.98 us (3%)
  starting transfers between devices  2.73 us (2%)
    pallas_call x1, Pallas kernels, run_main(): pl.pallas_call(main_kernel, name='moe_main', out_shape=(jax.ShapeDtypeStr...  73.4 us
    pallas_call x1, Pallas kernels, run_gate_up(): pl.pallas_call(gate_up_kernel, name='moe_dw_gate_up', in_specs=[anys, any...  18.4 us
    ppermute x1, waiting for transfers between devices, device_step(): r1 = perm(s1, perm=exchange_pairs('prim'))  13.4 us
    pallas_call x1, Pallas kernels, run_down(): pl.pallas_call(down_kernel, name='moe_dw_down', in_specs=[anys, anys], ou...  12.1 us
    unnamed x4, local copies, waits for them, and re-layouts  3.98 us
  transfers between devices with their start and end apart: 2, of which 1 were waited for; matrix products, arithmetic and copies ran while one was open for 0% of the time, Pallas kernels for 24%

profile of v3, /device:TPU:0, one launch (start us, length us, event | category | flops | bytes accessed | tf_op | source)
XLA Modules:
  0.0 128.7 jit_solution(11345923749340675016)
XLA Ops:
  0.6 73.4 %moe_main.1 = (bf16[64,2048]{1,0:T(8,128)(2,1)}, f32[6,64]{1,0:T(8,128)}, f32[2,64,2048]{2,1,0:T(8,128)}, f32[64,2048]{1,0:T(8,128)}, f32[64,2048]{1,0:T(8,128)}...) custom-call(bf16[64,2048]{1,0:T(8,128)(2,1)} %x_hbm.1, ...), custom_call_target="tpu_custom_call" | custom-call | flops 26575110144 | bytes 120000000 | tf_op jit(solution)/shard_map/moe_main/pallas_call | solution.py:431
  74.0 1.7 %collective-permute-start = (f32[2,64,2048]{2,1,0:T(8,128)}, f32[2,64,2048]{2,1,0:T(8,128)S(1)}, u32[]{:S(2)}, u32[]{:S(2)}) collective-permute-start(f32[2,64,2048]{2,1,0:T(8,128)} %get-tuple-element.19), channel_id=1, source_target_pairs={{0,2},{1,5},{2,0},{3,7},{4,6},{5,1},{6,4},{7,3}} | collective-permute-start | bytes 3145736 | tf_op jit(solution)/shard_map/ppermute | solution.py:590
  75.7 13.4 %collective-permute-done = f32[2,64,2048]{2,1,0:T(8,128)S(1)} collective-permute-done((f32[2,64,2048]{2,1,0:T(8,128)}, f32[2,64,2048]{2,1,0:T(8,128)S(1)}, u32[]{:S(2)}, u32[]{:S(2)}) %collective-permute-start) | collective-permute-done | bytes 1048608 | tf_op jit(solution)/shard_map/ppermute | solution.py:590
  89.0 0.0 copy-start
  89.1 1.0 copy-done
  90.1 1.9 %fusion = f32[64,2048]{1,0:T(8,128)} fusion(f32[64,2048]{1,0:T(8,128)} %get-tuple-element.20, f32[2,64,2048]{2,1,0:T(8,128)S(1)} %collective-permute-done), kind=kLoop, calls=%fused_computation.1 | loop fusion | flops 131072 | bytes 1572864 | tf_op jit(solution)/shard_map/add | solution.py:593
  92.0 1.1 collective-permute-start.1
  93.1 18.4 %moe_dw_gate_up.1 = (bf16[4,2048,1408]{2,1,0:T(8,128)(2,1)}, bf16[4,2048,1408]{2,1,0:T(8,128)(2,1)}) custom-call(bf16[4,192,2048]{2,1,0:T(8,128)(2,1)} %get-tuple-element.22.x_hbm, bf16[4,192,2816]{2,1,0:T(8,128)(2,1)} %get-tuple-element.23.g_hbm), custom_call_target="tpu_custom_call" | custom-call | flops 8858370048 | bytes 55000000 | tf_op jit(solution)/shard_map/moe_dw_gate_up/pallas_call | solution.py:515
  111.5 12.1 %moe_dw_down.1 = bf16[4,1408,2048]{2,1,0:T(8,128)(2,1)} custom-call(bf16[4,192,1408]{2,1,0:T(8,128)(2,1)} %get-tuple-element.26.h_hbm, bf16[4,192,2048]{2,1,0:T(8,128)(2,1)} %get-tuple-element.27.u_hbm), custom_call_target="tpu_custom_call" | custom-call | flops 4429185024 | bytes 28000000 | tf_op jit(solution)/shard_map/moe_dw_down/pallas_call | solution.py:559
  123.6 0.0 collective-permute-done.1
  123.6 2.1 %fusion.3 = bf16[64,2048]{1,0:T(8,128)(2,1)} fusion(f32[64,2048]{1,0:T(8,128)} %collective-permute-done.1, f32[64,2048]{1,0:T(8,128)} %get-tuple-element.18, f32[2,64,2048]{2,1,0:T(8,128)} %copy-done), kind=kLoop, calls=%fused_computation.5 | loop fusion | flops 393216 | bytes 1835008 | tf_op jit(solution)/shard_map/convert_element_type | solution.py:594
  125.7 1.7 %copy.15 = bf16[64,2048]{1,0:T(8,128)(2,1)} copy(bf16[64,2048]{1,0:T(8,128)(2,1)} %get-tuple-element.34) | data formatting | bytes 524288
  127.4 1.3 copy.16
Async XLA Ops:
  74.0 15.0 %collective-permute-start = (f32[2,64,2048]{2,1,0:T(8,128)}, f32[2,64,2048]{2,1,0:T(8,128)S(1)}, u32[]{:S(2)}, u32[]{:S(2)}) collective-permute-start(f32[2,64,2048]{2,1,0:T(8,128)} %get-tuple-element.19), channel_id=1, source_target_pairs={{0,2},{1,5},{2,0},{3,7},{4,6},{5,1},{6,4},{7,3}} | collective-permute-start | bytes 3145736 | tf_op jit(solution)/shard_map/ppermute | solution.py:590
  89.0 1.0 copy-start
  92.0 31.6 %collective-permute-start.1 = (f32[64,2048]{1,0:T(8,128)}, f32[64,2048]{1,0:T(8,128)}, u32[]{:S(2)}, u32[]{:S(2)}) collective-permute-start(f32[64,2048]{1,0:T(8,128)} %fusion), channel_id=1, source_target_pairs={{0,4},{1,3},{2,6},{3,1},{4,0},{5,7},{6,2},{7,5}} | collective-permute-start | bytes 1572872 | tf_op jit(solution)/shard_map/ppermute | solution.py:593

commit v4 on v3

--- a/solution.py
+++ b/solution.py
@@ -479,7 +479,10 @@
             cpy.wait()
 
 
-def gate_up_kernel(x_hbm, g_hbm, og_hbm, ou_hbm, x_v, g_v, og_v, ou_v, isem, osem):
+def gate_up_kernel(x_hbm, g_hbm, y_hbm, dg_hbm, og_hbm, ou_hbm, oy_hbm, odg_hbm,
+                   x_v, g_v, og_v, ou_v, y_v, dg_v, isem, osem, psem):
+    through = ((y_hbm, y_v, oy_hbm), (dg_hbm, dg_v, odg_hbm))
+
     def ins(e):
         return (pltpu.make_async_copy(x_hbm.at[e], x_v.at[e], isem.at[e, 0]),
                 pltpu.make_async_copy(g_hbm.at[e], g_v.at[e], isem.at[e, 1]))
@@ -501,27 +504,42 @@
             for cpy in ins(e):
                 cpy.wait()
 
+        @pl.when(i == 4)
+        def _():
+            for k, (src, mid, _) in enumerate(through):
+                pltpu.make_async_copy(src, mid, psem.at[k, 0]).start()
+
+        @pl.when(i == 8)
+        def _():
+            for k, (src, mid, dst) in enumerate(through):
+                pltpu.make_async_copy(src, mid, psem.at[k, 0]).wait()
+                pltpu.make_async_copy(mid, dst, psem.at[k, 1]).start()
+
         cols = pl.ds(pl.multiple_of(lax.rem(i, 4) * 512, 512), 512)
         r = dot(x_v[e, :, cols], g_v[e], TN)
         og_v[slot] = r[:, :F].astype(BF16)
         ou_v[slot] = r[:, F:].astype(BF16)
 
     ring_loop(4 * E, RING, outs, compute)
-
-
-def run_gate_up(xs, dgu):
+    for k, (_, mid, dst) in enumerate(through):
+        pltpu.make_async_copy(mid, dst, psem.at[k, 1]).wait()
+
+
+def run_gate_up(xs, dgu, y, dgt):
     anys = pl.BlockSpec(memory_space=pl.ANY)
     V = pltpu.VMEM
     return pl.pallas_call(
         gate_up_kernel, name='moe_dw_gate_up',
-        in_specs=[anys, anys], out_specs=(anys, anys),
-        out_shape=(jax.ShapeDtypeStruct((E, D, F), BF16),) * 2,
+        in_specs=[anys] * 4, out_specs=(anys,) * 4,
+        out_shape=(jax.ShapeDtypeStruct((E, D, F), BF16),) * 2
+        + (jax.ShapeDtypeStruct((TD, D), BF16), jax.ShapeDtypeStruct((K, TD), F32)),
         scratch_shapes=[V((E, ROWS, D), BF16), V((E, ROWS, 2 * F), BF16),
-                        V((RING, 512, F), BF16), V((RING, 512, F), BF16),
-                        pltpu.SemaphoreType.DMA((E, 2)), pltpu.SemaphoreType.DMA((RING, 2))],
+                        V((RING, 512, F), BF16), V((RING, 512, F), BF16), V((TD, D), BF16), V((K, TD), F32),
+                        pltpu.SemaphoreType.DMA((E, 2)), pltpu.SemaphoreType.DMA((RING, 2)),
+                        pltpu.SemaphoreType.DMA((2, 2))],
         compiler_params=pltpu.CompilerParams(vmem_limit_bytes=67043328),
         cost_estimate=pl.CostEstimate(flops=4 * E * ROWS * D * F, bytes_accessed=55_000_000, transcendentals=0),
-    )(xs, dgu)
+    )(xs, dgu, y, dgt)
 
 
 def down_kernel(h_hbm, u_hbm, o_hbm, h_v, u_v, ht_v, o_v, isem, osem):
@@ -534,15 +552,19 @@
             cpy.start()
 
     def cols(i):
-        return pl.ds(pl.multiple_of(lax.rem(i, 4) * 512, 512), 512)
+        return pl.ds(pl.multiple_of(lax.rem(i, 2) * 1024, 1024), 1024)
 
     def outs(i, slot):
-        return (pltpu.make_async_copy(o_v.at[slot], o_hbm.at[i // 4, :, cols(i)], osem.at[slot]),)
+        halves = []
+        for k in range(2):
+            rows = pl.ds(704 * k, 704)
+            halves.append(pltpu.make_async_copy(o_v.at[slot, rows], o_hbm.at[i // 2, rows, cols(i)], osem.at[slot, k]))
+        return halves
 
     def compute(i, slot):
-        e = i // 4
-
-        @pl.when(lax.rem(i, 4) == 0)
+        e = i // 2
+
+        @pl.when(lax.rem(i, 2) == 0)
         def _():
             for cpy in ins(e):
                 cpy.wait()
@@ -550,7 +572,7 @@
 
         o_v[slot] = dot(ht_v[...], u_v[e, :, cols(i)]).astype(BF16)
 
-    ring_loop(4 * E, RING, outs, compute)
+    ring_loop(2 * E, RING, outs, compute)
 
 
 def run_down(hs, us):
@@ -560,8 +582,8 @@
         down_kernel, name='moe_dw_down',
         in_specs=[anys, anys], out_specs=anys,
         out_shape=jax.ShapeDtypeStruct((E, F, D), BF16),
-        scratch_shapes=[V((E, ROWS, F), BF16), V((E, ROWS, D), BF16), V((F, ROWS), BF16), V((RING, F, 512), BF16),
-                        pltpu.SemaphoreType.DMA((E, 2)), pltpu.SemaphoreType.DMA((RING,))],
+        scratch_shapes=[V((E, ROWS, F), BF16), V((E, ROWS, D), BF16), V((F, ROWS), BF16), V((RING, F, 1024), BF16),
+                        pltpu.SemaphoreType.DMA((E, 2)), pltpu.SemaphoreType.DMA((RING, 2))],
         compiler_params=pltpu.CompilerParams(vmem_limit_bytes=67043328),
         cost_estimate=pl.CostEstimate(flops=2 * E * ROWS * D * F, bytes_accessed=28_000_000, transcendentals=0),
     )(hs, us)
@@ -588,7 +610,7 @@
         layer_out, dgt, s1, own, second, xs, us, hs, dgu = run_main(tok, dy, idx.T, gate.T, wg, wu, wd)
         perm = functools.partial(lax.ppermute, axis_name=('ei', 'eo'))
         r1 = perm(s1, perm=exchange_pairs('prim'))
-        g_gate, g_up = run_gate_up(xs, dgu)
+        g_gate, g_up, layer_out, dgt = run_gate_up(xs, dgu, layer_out, dgt)
         g_down = run_down(hs, us)
         r2 = perm(second + r1[1], perm=exchange_pairs('sec'))
         grad_tok = (own + r1[0] + r2).astype(BF16)

time: 129 us -> 125 us (0.969)
  local copies, waits for them, and re-layouts: 3.98 us -> 1.04 us
    unnamed x4 -> x2, local copies, waits for them, and re-layouts: 3.98 us -> 1.04 us
where the time goes in v4:
time: 125 us
  Pallas kernels  103 us (82%)
  waiting for transfers between devices  13.4 us (11%)
  other arithmetic  4.05 us (3%)
  starting transfers between devices  2.73 us (2%)
    pallas_call x1, Pallas kernels, run_main(): pl.pallas_call(main_kernel, name='moe_main', out_shape=(jax.ShapeDtypeStr...  73.4 us
    pallas_call x1, Pallas kernels, run_gate_up(): pl.pallas_call(gate_up_kernel, name='moe_dw_gate_up', in_specs=[anys] * 4...  18.5 us
    ppermute x1, waiting for transfers between devices, device_step(): r1 = perm(s1, perm=exchange_pairs('prim'))  13.4 us
    pallas_call x1, Pallas kernels, run_down(): pl.pallas_call(down_kernel, name='moe_dw_down', in_specs=[anys, anys], ou...  11.3 us
  transfers between devices with their start and end apart: 2, of which 1 were waited for; matrix products, arithmetic and copies ran while one was open for 0% of the time, Pallas kernels for 24%

profile of v4, /device:TPU:0, one launch (start us, length us, event | category | flops | bytes accessed | tf_op | source)
XLA Modules:
  0.0 125.0 jit_solution(7596797157967029150)
XLA Ops:
  0.6 73.4 %moe_main.1 = (bf16[64,2048]{1,0:T(8,128)(2,1)}, f32[6,64]{1,0:T(8,128)}, f32[2,64,2048]{2,1,0:T(8,128)}, f32[64,2048]{1,0:T(8,128)}, f32[64,2048]{1,0:T(8,128)}...) custom-call(bf16[64,2048]{1,0:T(8,128)(2,1)} %x_hbm.1, ...), custom_call_target="tpu_custom_call" | custom-call | flops 26575110144 | bytes 120000000 | tf_op jit(solution)/shard_map/moe_main/pallas_call | solution.py:431
  74.0 1.7 %collective-permute-start = (f32[2,64,2048]{2,1,0:T(8,128)}, f32[2,64,2048]{2,1,0:T(8,128)S(1)}, u32[]{:S(2)}, u32[]{:S(2)}) collective-permute-start(f32[2,64,2048]{2,1,0:T(8,128)} %get-tuple-element.25), channel_id=1, source_target_pairs={{0,2},{1,5},{2,0},{3,7},{4,6},{5,1},{6,4},{7,3}} | collective-permute-start | bytes 3145736 | tf_op jit(solution)/shard_map/ppermute | solution.py:612
  75.7 13.4 %collective-permute-done = f32[2,64,2048]{2,1,0:T(8,128)S(1)} collective-permute-done((f32[2,64,2048]{2,1,0:T(8,128)}, f32[2,64,2048]{2,1,0:T(8,128)S(1)}, u32[]{:S(2)}, u32[]{:S(2)}) %collective-permute-start) | collective-permute-done | bytes 1048608 | tf_op jit(solution)/shard_map/ppermute | solution.py:612
  89.0 0.0 copy-start
  89.1 1.0 copy-done
  90.1 1.9 %fusion = f32[64,2048]{1,0:T(8,128)} fusion(f32[64,2048]{1,0:T(8,128)} %get-tuple-element.26, f32[2,64,2048]{2,1,0:T(8,128)S(1)} %collective-permute-done), kind=kLoop, calls=%fused_computation.1 | loop fusion | flops 131072 | bytes 1572864 | tf_op jit(solution)/shard_map/add | solution.py:615
  92.0 1.1 collective-permute-start.1
  93.1 18.5 %moe_dw_gate_up.1 = (bf16[4,2048,1408]{2,1,0:T(8,128)(2,1)}, bf16[4,2048,1408]{2,1,0:T(8,128)(2,1)}, bf16[64,2048]{1,0:T(8,128)(2,1)}, f32[6,64]{1,0:T(8,128)}) custom-call(bf16[4,192,2048]{2,1,0:T(8,128)(2,1)} %get-tuple-element.19.x_hbm, bf16[4,192,2816]{2,1,0:T(8,128)(2,1)} %get-tuple-element.20.g_hbm, bf16[64,2048]{1,0:T(8,128)(2,1)} %get-tuple-element.21.y_hbm, ...), custom_call_target="tpu_custom_call" | custom-call | flops 8858370048 | bytes 55000000 | tf_op jit(solution)/shard_map/moe_dw_gate_up/pallas_call | solution.py:531
  111.6 11.3 %moe_dw_down.1 = bf16[4,1408,2048]{2,1,0:T(8,128)(2,1)} custom-call(bf16[4,192,1408]{2,1,0:T(8,128)(2,1)} %get-tuple-element.30.h_hbm, bf16[4,192,2048]{2,1,0:T(8,128)(2,1)} %get-tuple-element.31.u_hbm), custom_call_target="tpu_custom_call" | custom-call | flops 4429185024 | bytes 28000000 | tf_op jit(solution)/shard_map/moe_dw_down/pallas_call | solution.py:581
  122.9 0.0 collective-permute-done.1
  122.9 2.1 %fusion.3 = bf16[64,2048]{1,0:T(8,128)(2,1)} fusion(f32[64,2048]{1,0:T(8,128)} %collective-permute-done.1, f32[64,2048]{1,0:T(8,128)} %get-tuple-element.24, f32[2,64,2048]{2,1,0:T(8,128)} %copy-done), kind=kLoop, calls=%fused_computation.5 | loop fusion | flops 393216 | bytes 1835008 | tf_op jit(solution)/shard_map/convert_element_type | solution.py:616
Async XLA Ops:
  74.0 15.0 %collective-permute-start = (f32[2,64,2048]{2,1,0:T(8,128)}, f32[2,64,2048]{2,1,0:T(8,128)S(1)}, u32[]{:S(2)}, u32[]{:S(2)}) collective-permute-start(f32[2,64,2048]{2,1,0:T(8,128)} %get-tuple-element.25), channel_id=1, source_target_pairs={{0,2},{1,5},{2,0},{3,7},{4,6},{5,1},{6,4},{7,3}} | collective-permute-start | bytes 3145736 | tf_op jit(solution)/shard_map/ppermute | solution.py:612
  89.0 1.0 copy-start
  92.0 30.9 %collective-permute-start.1 = (f32[64,2048]{1,0:T(8,128)}, f32[64,2048]{1,0:T(8,128)}, u32[]{:S(2)}, u32[]{:S(2)}) collective-permute-start(f32[64,2048]{1,0:T(8,128)} %fusion), channel_id=1, source_target_pairs={{0,4},{1,3},{2,6},{3,1},{4,0},{5,7},{6,2},{7,5}} | collective-permute-start | bytes 1572872 | tf_op jit(solution)/shard_map/ppermute | solution.py:615

commit v5 on v4

--- a/solution.py
+++ b/solution.py
@@ -147,8 +147,9 @@
     ag_open(2)
     ag_open(3)
     ins[3].wait()
-    start_gate_up(0, 0)
-    start_down(0, 0)
+    for e in range(2):
+        start_gate_up(e, e)
+        start_down(e, e)
     for step in (ag_first, ag_second, ag_diag):
         for st in range(2):
             step(st)
@@ -192,8 +193,6 @@
 
     ag_diag(2)
     ag_diag(3)
-    start_gate_up(1, 1)
-    start_down(1, 1)
     ag_open(4)
     ag_last(2)
     ag_last(3)

time: 125 us -> 125 us (level)
  no operation moved by 1% of the time
where the time goes in v5:
time: 125 us
  Pallas kernels  103 us (82%)
  waiting for transfers between devices  13.4 us (11%)
  other arithmetic  4.05 us (3%)
  starting transfers between devices  2.61 us (2%)
    pallas_call x1, Pallas kernels, run_main(): pl.pallas_call(main_kernel, name='moe_main', out_shape=(jax.ShapeDtypeStr...  73.4 us
    pallas_call x1, Pallas kernels, run_gate_up(): pl.pallas_call(gate_up_kernel, name='moe_dw_gate_up', in_specs=[anys] * 4...  18.5 us
    ppermute x1, waiting for transfers between devices, device_step(): r1 = perm(s1, perm=exchange_pairs('prim'))  13.4 us
    pallas_call x1, Pallas kernels, run_down(): pl.pallas_call(down_kernel, name='moe_dw_down', in_specs=[anys, anys], ou...  11.3 us
  transfers between devices with their start and end apart: 2, of which 1 were waited for; matrix products, arithmetic and copies ran while one was open for 0% of the time, Pallas kernels for 24%

profile of v5, /device:TPU:0, one launch (start us, length us, event | category | flops | bytes accessed | tf_op | source)
XLA Modules:
  0.0 124.9 jit_solution(688304690919518731)
XLA Ops:
  0.6 73.4 %moe_main.1 = (bf16[64,2048]{1,0:T(8,128)(2,1)}, f32[6,64]{1,0:T(8,128)}, f32[2,64,2048]{2,1,0:T(8,128)}, f32[64,2048]{1,0:T(8,128)}, f32[64,2048]{1,0:T(8,128)}...) custom-call(bf16[64,2048]{1,0:T(8,128)(2,1)} %x_hbm.1, ...), custom_call_target="tpu_custom_call" | custom-call | flops 26575110144 | bytes 120000000 | tf_op jit(solution)/shard_map/moe_main/pallas_call | solution.py:430
  74.0 1.6 %collective-permute-start = (f32[2,64,2048]{2,1,0:T(8,128)}, f32[2,64,2048]{2,1,0:T(8,128)S(1)}, u32[]{:S(2)}, u32[]{:S(2)}) collective-permute-start(f32[2,64,2048]{2,1,0:T(8,128)} %get-tuple-element.25), channel_id=1, source_target_pairs={{0,2},{1,5},{2,0},{3,7},{4,6},{5,1},{6,4},{7,3}} | collective-permute-start | bytes 3145736 | tf_op jit(solution)/shard_map/ppermute | solution.py:611
  75.7 13.4 %collective-permute-done = f32[2,64,2048]{2,1,0:T(8,128)S(1)} collective-permute-done((f32[2,64,2048]{2,1,0:T(8,128)}, f32[2,64,2048]{2,1,0:T(8,128)S(1)}, u32[]{:S(2)}, u32[]{:S(2)}) %collective-permute-start) | collective-permute-done | bytes 1048608 | tf_op jit(solution)/shard_map/ppermute | solution.py:611
  89.0 0.0 copy-start
  89.0 1.0 copy-done
  90.1 1.9 %fusion = f32[64,2048]{1,0:T(8,128)} fusion(f32[64,2048]{1,0:T(8,128)} %get-tuple-element.26, f32[2,64,2048]{2,1,0:T(8,128)S(1)} %collective-permute-done), kind=kLoop, calls=%fused_computation.1 | loop fusion | flops 131072 | bytes 1572864 | tf_op jit(solution)/shard_map/add | solution.py:614
  92.0 1.0 collective-permute-start.1
  93.0 18.5 %moe_dw_gate_up.1 = (bf16[4,2048,1408]{2,1,0:T(8,128)(2,1)}, bf16[4,2048,1408]{2,1,0:T(8,128)(2,1)}, bf16[64,2048]{1,0:T(8,128)(2,1)}, f32[6,64]{1,0:T(8,128)}) custom-call(bf16[4,192,2048]{2,1,0:T(8,128)(2,1)} %get-tuple-element.19.x_hbm, bf16[4,192,2816]{2,1,0:T(8,128)(2,1)} %get-tuple-element.20.g_hbm, bf16[64,2048]{1,0:T(8,128)(2,1)} %get-tuple-element.21.y_hbm, ...), custom_call_target="tpu_custom_call" | custom-call | flops 8858370048 | bytes 55000000 | tf_op jit(solution)/shard_map/moe_dw_gate_up/pallas_call | solution.py:530
  111.5 11.3 %moe_dw_down.1 = bf16[4,1408,2048]{2,1,0:T(8,128)(2,1)} custom-call(bf16[4,192,1408]{2,1,0:T(8,128)(2,1)} %get-tuple-element.30.h_hbm, bf16[4,192,2048]{2,1,0:T(8,128)(2,1)} %get-tuple-element.31.u_hbm), custom_call_target="tpu_custom_call" | custom-call | flops 4429185024 | bytes 28000000 | tf_op jit(solution)/shard_map/moe_dw_down/pallas_call | solution.py:580
  122.8 0.0 collective-permute-done.1
  122.8 2.1 %fusion.3 = bf16[64,2048]{1,0:T(8,128)(2,1)} fusion(f32[64,2048]{1,0:T(8,128)} %collective-permute-done.1, f32[64,2048]{1,0:T(8,128)} %get-tuple-element.24, f32[2,64,2048]{2,1,0:T(8,128)} %copy-done), kind=kLoop, calls=%fused_computation.5 | loop fusion | flops 393216 | bytes 1835008 | tf_op jit(solution)/shard_map/convert_element_type | solution.py:615
Async XLA Ops:
  74.0 15.0 %collective-permute-start = (f32[2,64,2048]{2,1,0:T(8,128)}, f32[2,64,2048]{2,1,0:T(8,128)S(1)}, u32[]{:S(2)}, u32[]{:S(2)}) collective-permute-start(f32[2,64,2048]{2,1,0:T(8,128)} %get-tuple-element.25), channel_id=1, source_target_pairs={{0,2},{1,5},{2,0},{3,7},{4,6},{5,1},{6,4},{7,3}} | collective-permute-start | bytes 3145736 | tf_op jit(solution)/shard_map/ppermute | solution.py:611
  89.0 1.0 copy-start
  92.0 30.8 %collective-permute-start.1 = (f32[64,2048]{1,0:T(8,128)}, f32[64,2048]{1,0:T(8,128)}, u32[]{:S(2)}, u32[]{:S(2)}) collective-permute-start(f32[64,2048]{1,0:T(8,128)} %fusion), channel_id=1, source_target_pairs={{0,4},{1,3},{2,6},{3,1},{4,0},{5,7},{6,2},{7,5}} | collective-permute-start | bytes 1572872 | tf_op jit(solution)/shard_map/ppermute | solution.py:614
